TPU v7x, 8 devices: a whole 2x2x1 slice. The times are simulated.
8 devices in a mesh: data: 1 (over z), outer: 2 (over y), expert: 4 (over x, core).
Axes of the slice: x: 2, y: 2, z: 1, core: 2. Of those that a mesh axis runs over, the one named last changes fastest.
Arguments:
- x: bfloat16 [2048, 2048], P(('data', 'outer', 'expert'))
- wr: bfloat16 [2048, 128], replicated
- idx: int32 [2048, 8], P(('data', 'outer', 'expert'))
- w1: bfloat16 [128, 2048, 768], P(('outer', 'expert'))
- w3: bfloat16 [128, 2048, 768], P(('outer', 'expert'))
- w2: bfloat16 [128, 768, 2048], P(('outer', 'expert'))
Outputs:
- output: bfloat16 [2048, 2048], P(('data', 'outer', 'expert'))
All inputs are finite; a program needn't handle non-finite values.
Results may differ from a plain program's by a relative error of at most 0.00813279.
Values are sent between devices in bfloat16 or wider.
A program may use at most 1 GiB of HBM per device.

v0:
```python
import jax
import jax.numpy as jnp
from jax import lax
from jax.sharding import PartitionSpec as P


def _gate(x, wr, idx):
    logits = jnp.dot(x, wr, preferred_element_type=jnp.float32)
    oh = idx[:, :, None] == jnp.arange(wr.shape[1], dtype=idx.dtype)
    return jax.nn.softmax(jnp.sum(jnp.where(oh, logits[:, None, :], 0.0), axis=-1), axis=-1)


def _plan(idx, g, base, ne, cap):
    t = idx.shape[-2]
    oh = idx[..., None] == base + jnp.arange(ne, dtype=idx.dtype)
    m = jnp.sum(oh, axis=-2, dtype=jnp.int32).astype(jnp.float32)
    pos = jnp.arange(t, dtype=jnp.int32)
    tri = (pos[None, :] < pos[:, None]).astype(jnp.bfloat16)
    cnt = jnp.einsum('uv,...ve->...ue', tri, m.astype(jnp.bfloat16), preferred_element_type=jnp.float32)
    c = jnp.arange(cap, dtype=jnp.float32)
    hit = (c >= cnt[..., None]) & (c < (cnt + m)[..., None])
    ge = jnp.sum(jnp.where(oh, g[..., None], 0.0), axis=-2)
    w = jnp.where(hit, ge[..., None], 0.0)
    return hit.astype(jnp.bfloat16), w


def _split(w):
    hi = w.astype(jnp.bfloat16)
    r = w - hi.astype(jnp.float32)
    mid = r.astype(jnp.bfloat16)
    lo = (r - mid.astype(jnp.float32)).astype(jnp.bfloat16)
    return jnp.stack([hi, mid, lo])


def solution(mesh):
    O = mesh.shape['outer']
    X = mesh.shape['expert']
    n = O * X
    tok = P(('data', 'outer', 'expert'), None)
    wsp = P(('outer', 'expert'), None, None)

    def local(x, wr, idx, w1, w3, w2):
        T, dm = x.shape
        k = idx.shape[1]
        E = wr.shape[1]
        el = w1.shape[0]
        C = 2 * T * k // E
        g = _gate(x, wr, idx)
        hit, w = _plan(idx, g, 0, E, C)
        ws = _split(w).reshape(3 * T, E * C)
        buf = jnp.einsum('tec,td->ecd', hit, x, preferred_element_type=jnp.float32).astype(x.dtype)
        buf = buf.reshape(O, X, el * C, dm)
        buf = lax.all_to_all(buf, 'expert', 1, 1, tiled=True)
        buf = lax.all_to_all(buf, 'outer', 0, 0, tiled=True)
        xin = buf.reshape(n, el, C, dm).transpose(1, 0, 2, 3).reshape(el, n * C, dm)
        a = jnp.einsum('ecd,edf->ecf', xin, w1, preferred_element_type=jnp.float32)
        b = jnp.einsum('ecd,edf->ecf', xin, w3, preferred_element_type=jnp.float32)
        h = (jax.nn.silu(a) * b).astype(jnp.bfloat16)
        o = jnp.einsum('ecf,efd->ecd', h, w2, preferred_element_type=jnp.float32).astype(jnp.bfloat16)
        o = o.reshape(el, n, C, dm).transpose(1, 0, 2, 3).reshape(O, X, el * C, dm)
        o = lax.all_to_all(o, 'outer', 0, 0, tiled=True)
        o = lax.all_to_all(o, 'expert', 1, 1, tiled=True)
        y = jnp.dot(ws, o.reshape(E * C, dm), preferred_element_type=jnp.float32)
        return jnp.sum(y.reshape(3, T, dm), axis=0).astype(jnp.bfloat16)

    return jax.shard_map(local, mesh=mesh, in_specs=(tok, P(None, None), tok, wsp, wsp, wsp), out_specs=tok, check_vma=False)
```

profile of v0, /device:TPU:0, one launch (start us, length us, event | category | flops | bytes accessed | tf_op | source)
XLA Modules:
  0.0 902.3 jit_solution(4096843297111935712)
XLA Ops:
  2.6 8.5 convolution_convert_fusion.1
  11.1 15.1 %copy.66 = bf16[128,32,2048]{2,1,0:T(8,128)(2,1)S(1)} copy(bf16[128,32,2048]{2,0,1:T(8,128)(2,1)} %convolution_convert_fusion.1) | data formatting | bytes 33554432 | tf_op jit(solution)/shard_map/convert_element_type | solution.py:51
  26.3 2.5 copy.67
  28.8 187.4 %all_to_all.20 = bf16[2,4,512,2048]{3,2,0,1:T(8,128)(2,1)S(1)} all-to-all(bf16[2,4,512,2048]{3,2,0,1:T(8,128)(2,1)S(1)} %copy.67), channel_id=1, replica_groups=mesh['data'=1,'outer'=2,'expert'=4] {'expert'}, dimensions={1} | all-to-all | bytes 33554432 | tf_op jit(solution)/shard_map/all_to_all | solution.py:53
  216.2 2.4 copy.68
  218.6 186.4 %all_to_all.21 = bf16[2,4,512,2048]{3,2,1,0:T(8,128)(2,1)S(1)} all-to-all(bf16[2,4,512,2048]{3,2,1,0:T(8,128)(2,1)S(1)} %copy.68), channel_id=1, replica_groups=mesh['data'=1,'outer'=2,'expert'=4] {'outer'}, dimensions={0} | all-to-all | bytes 33554432 | tf_op jit(solution)/shard_map/all_to_all | solution.py:54
  405.0 6.6 copy.69
  411.6 28.5 %fusion.23 = f32[16,256,768]{2,1,0:T(8,128)} fusion(bf16[16,256,2048]{2,1,0:T(8,128)(2,1)} %bitcast.35, bf16[16,2048,768]{2,1,0:T(8,128)(2,1)} %param.9), kind=kOutput, calls=%fused_computation.36 | convolution fusion | flops 12884901888 | bytes 79691776 | tf_op jit(solution)/shard_map/ecd,edf->ecf/dot_general | solution.py:56
  440.1 47.7 %convolution_convert_fusion = bf16[16,256,2048]{2,1,0:T(8,128)(2,1)} fusion(bf16[16,768,2048]{2,1,0:T(8,128)(2,1)} %param.11, f32[16,256,768]{2,1,0:T(8,128)} %fusion.23, bf16[16,256,2048]{2,1,0:T(8,128)(2,1)} %bitcast.36, bf16[16,2048,768]{2,1,0:T(8,128)(2,1)} %param.10), kind=kOutput, calls=%fused_computation | convolution fusion | flops 25797066752 | bytes 146800640 | tf_op jit(solution)/shard_map/ecf,efd->ecd/dot_general | solution.py:59
  487.8 8.0 copy.70
  495.9 185.3 %all_to_all.22 = bf16[2,4,512,2048]{3,2,1,0:T(8,128)(2,1)S(1)} all-to-all(bf16[2,4,512,2048]{3,2,1,0:T(8,128)(2,1)S(1)} %bitcast.33), channel_id=1, replica_groups=mesh['data'=1,'outer'=2,'expert'=4] {'outer'}, dimensions={0} | all-to-all | bytes 33554432 | tf_op jit(solution)/shard_map/all_to_all | solution.py:61
  681.2 6.6 copy.71
  687.7 7.3 all-to-all-start.3
  698.1 2.3 broadcast_in_dim.54
  700.4 5.6 copy.64
  706.0 2.2 lt.49
  708.3 5.6 copy.59
  713.9 2.3 ge.52
  716.2 5.6 copy.57
  721.9 7.2 fusion.21
  729.1 2.8 fusion.9
  731.9 145.7 %all-to-all-done.3 = bf16[2,4,512,2048]{3,2,0,1:T(8,128)(2,1)} async-done(((bf16[2,4,512,2048]{3,2,0,1:T(8,128)(2,1)}), bf16[2,4,512,2048]{3,2,0,1:T(8,128)(2,1)}, u32[]{:S(2)}, u32[]{:S(2)}) %all-to-all-start.3) | async-done | bytes 16777248 | tf_op jit(solution)/shard_map/all_to_all | solution.py:62
  877.5 8.0 copy.72
  885.6 16.8 %fusion.10 = bf16[256,2048]{1,0:T(8,128)(2,1)} fusion(bf16[4096,2048,1]{1,0,2:T(8,128)(2,1)S(1)} %bitcast.34, bf16[1,256,4096]{2,1,0:T(8,128)(2,1)} %get-tuple-element.8, bf16[1,256,4096]{2,1,0:T(8,128)(2,1)} %get-tuple-element.7, bf16[1,256,4096]{2,1,0:T(8,128)(2,1)} %get-tuple-element.5), kind=kOutput, calls=%fused_computation.18 | convolution fusion | flops 12892241920 | bytes 24117248 | tf_op jit(solution)/shard_map/dot_general | solution.py:63
  (33 shorter events, 5.6 us)
Async XLA Ops:
  0.0 2.6 copy-start
  0.9 0.7 copy-start.1
  1.6 24.6 %copy-start.5 = (f32[256,128]{0,1:T(8,128)}, f32[256,128]{0,1:T(8,128)S(1)}, u32[]{:S(2)}) copy-start(f32[256,128]{0,1:T(8,128)S(1)} %copy.58) | copy-start | bytes 393220
  1.7 24.5 %copy-start.3 = (f32[256,128]{0,1:T(8,128)}, f32[256,128]{0,1:T(8,128)S(1)}, u32[]{:S(2)}) copy-start(f32[256,128]{0,1:T(8,128)S(1)} %copy.56) | copy-start | bytes 393220
  687.7 7.3 copy-start.7
  687.7 7.8 copy-start.2
  687.7 189.8 %all-to-all-start.3 = ((bf16[2,4,512,2048]{3,2,0,1:T(8,128)(2,1)}), bf16[2,4,512,2048]{3,2,0,1:T(8,128)(2,1)}, u32[]{:S(2)}, u32[]{:S(2)}) async-start(bf16[2,4,512,2048]{3,2,0,1:T(8,128)(2,1)} %copy.71), calls=%async_computation.3 | async-start | bytes 33554432 | tf_op jit(solution)/shard_map/all_to_all | solution.py:62
  695.1 11.0 %copy-start.6 = (f32[256,128]{0,1:T(8,128)S(1)}, f32[256,128]{0,1:T(8,128)}, u32[]{:S(2)}) copy-start(f32[256,128]{0,1:T(8,128)} %copy-done.5) | copy-start | bytes 393220
  698.1 15.8 %copy-start.4 = (f32[256,128]{0,1:T(8,128)S(1)}, f32[256,128]{0,1:T(8,128)}, u32[]{:S(2)}) copy-start(f32[256,128]{0,1:T(8,128)} %copy-done.3) | copy-start | bytes 393220
where the time goes:
time: 903 us; the launch traced here: 902 us
  blocking collectives  559 us (62%)
  waiting for transfers between devices  146 us (16%)
  matrix products  102 us (11%)
  local copies, waits for them, and re-layouts  74.4 us (8%)
  other arithmetic  13.5 us (1%)
    all_to_all x1, blocking collectives, local(): buf = lax.all_to_all(buf, 'expert', 1, 1, tiled=True)  187 us
    all_to_all x1, blocking collectives, local(): buf = lax.all_to_all(buf, 'outer', 0, 0, tiled=True)  186 us
    all_to_all x1, blocking collectives, local(): o = lax.all_to_all(o, 'outer', 0, 0, tiled=True)  185 us
    all_to_all x1, waiting for transfers between devices, local(): o = lax.all_to_all(o, 'expert', 1, 1, tiled=True)  146 us
    dot_general x1, matrix products, local(): jnp.einsum('ecf,efd->ecd', h, w2, preferred_element_type=jnp.float32)  47.7 us
    dot_general x1, matrix products, local(): a = jnp.einsum('ecd,edf->ecf', xin, w1, preferred_element_type=jnp.float32)  28.5 us
  transfers between devices with their start and end apart: 1, of which 1 were waited for; matrix products, arithmetic and copies ran while one was open for 4% of the time, Pallas kernels for 0%

commit v1 on v0

v1 whole, which is shorter than its diff:
```python
import functools

import jax
import jax.numpy as jnp
from jax import lax
from jax.experimental import pallas as pl
from jax.experimental.pallas import tpu as pltpu
from jax.sharding import PartitionSpec as P

MESH = pl.DeviceIdType.MESH
BF = jnp.bfloat16
F32 = jnp.float32
U = 256
CW = 128
NWT = 3
NW2 = 4


def _dot(a, b):
    return jnp.dot(a, b, preferred_element_type=F32)


def kernel(x_hbm, wr_hbm, idx_hbm, w1_hbm, w3_hbm, w2_hbm, out_ref,
           X, WR, IDX, ET, EX, POS, HT, W, XIN, ACC, WT, W2T, OB,
           xsem, wtsem, w2sem, dsend, drecv, esend, erecv,
           d2s, d2r, p1s, p1r, p2s, p2r, ready):
    T, D = x_hbm.shape
    E = wr_hbm.shape[1]
    EL, _, FF = w1_hbm.shape
    K = idx_hbm.shape[1]
    C = 2 * T * K // E
    S = EL * C
    NU = D // U
    NQ = NU // 2
    NB = D // (2 * CW)
    NF = FF // U

    dd = lax.axis_index("data")
    oy = lax.axis_index("outer")
    jx = lax.axis_index("expert")
    cx = jx // 2
    cc = jx - 2 * cx
    nx = lax.axis_size("expert")

    def dev(r):
        ry, rx, rc = r // 4, (r // 2) % 2, r % 2
        y = 1 - oy if ry else oy
        x = 1 - cx if rx else cx
        c = 1 - cc if rc else cc
        return y, x * 2 + c

    def did(r):
        y, j = dev(r)
        return (dd, y, j)

    def pos_of(r):
        y, j = dev(r)
        return y * nx + j

    def xload(u):
        return pltpu.make_async_copy(x_hbm.at[:, pl.ds(u * U, U)], X.at[u * 8], xsem.at[u])

    wrload = pltpu.make_async_copy(wr_hbm, WR, xsem.at[NU])
    idxload = pltpu.make_async_copy(idx_hbm, IDX, xsem.at[NU + 1])

    def wtload(n, m):
        q, e, s = n // EL, n % EL, n % NWT
        src = w1_hbm if m == 0 else w3_hbm
        rows = pl.ds(pl.multiple_of(q * 2 * U, 2 * U), 2 * U)
        return pltpu.make_async_copy(src.at[e, rows, :], WT.at[s, m], wtsem.at[s, m])

    def w2load(n, m):
        b, e, s = n // EL, n % EL, n % NW2
        cols = pl.ds(pl.multiple_of(m * (D // 2) + b * CW, CW), CW)
        return pltpu.make_async_copy(w2_hbm.at[e, :, cols], W2T.at[s, :, pl.ds(m * CW, CW)], w2sem.at[s, m])

    H = T // 2

    def blk(u, r, half=None):
        b = u * 8 + r
        if half is None:
            return X.at[b]
        return X.at[b, pl.ds(half * H, H)]

    def disp(k, u):
        src, dst, to = [
            (blk(u, 0), blk(u, 2), 2), (blk(u, 0), blk(u, 4), 4), (blk(u, 0), blk(u, 1), 1),
            (blk(u, 2, 0), blk(u, 6, 0), 4), (blk(u, 4, 1), blk(u, 6, 1), 2),
            (blk(u, 2), blk(u, 3), 1), (blk(u, 4), blk(u, 5), 1), (blk(u, 6), blk(u, 7), 1),
        ][k]
        return pltpu.make_async_remote_copy(src_ref=src, dst_ref=dst, send_sem=dsend.at[k, u], recv_sem=drecv.at[k, u],
                                            device_id=did(to), device_id_type=MESH)

    def own(u):
        for k in (0, 1, 2):
            disp(k, u).start()

    def fwd(u):
        disp(0, u).wait_recv()
        disp(1, u).wait_recv()
        for k in (3, 4, 5, 6):
            disp(k, u).start()

    def diag(u):
        disp(3, u).wait_recv()
        disp(4, u).wait_recv()
        disp(7, u).start()

    def arrived(u):
        for k in (2, 5, 6, 7):
            disp(k, u).wait_recv()

    def sent(u):
        for k in range(8):
            disp(k, u).wait_send()

    def ecopy(r):
        rows = pl.ds(pl.multiple_of(pos_of(r) * EL, EL), EL)
        return pltpu.make_async_remote_copy(src_ref=ET.at[rows], dst_ref=EX.at[pl.ds(r * EL, EL)],
                                            send_sem=esend.at[r], recv_sem=erecv.at[r],
                                            device_id=did(r), device_id_type=MESH)

    for u in range(NU):
        xload(u).start()
    wrload.start()
    idxload.start()
    for n in range(NWT):
        wtload(n, 0).start()
        wtload(n, 1).start()

    barrier = pltpu.get_barrier_semaphore()
    for r in range(1, 8):
        pl.semaphore_signal(barrier, inc=1, device_id=did(r), device_id_type=MESH)
    xload(0).wait()
    pl.semaphore_wait(barrier, 7)
    own(0)

    for u in range(1, NU):
        xload(u).wait()
    wrload.wait()
    idxload.wait()
    logits = _dot(X[0], WR[0:U])
    for u in range(1, NU):
        logits = logits + _dot(X[u * 8], WR[u * U:(u + 1) * U])
    lane = lax.broadcasted_iota(jnp.int32, (T, E), 1)
    ids = IDX[...]
    chosen = lane == ids[:, 0:1]
    for j in range(1, K):
        chosen = chosen | (lane == ids[:, j:j + 1])
    top = jnp.max(jnp.where(chosen, logits, -jnp.inf), axis=1, keepdims=True)
    ex = jnp.where(chosen, jnp.exp(jnp.where(chosen, logits - top, 0.0)), 0.0)
    g = ex / jnp.sum(ex, axis=1, keepdims=True)
    ET[...] = jnp.transpose(jnp.where(chosen, g, -1.0))
    for r in range(1, 8):
        ecopy(r).start()
    own(1)

    @pl.loop(0, ACC.shape[0])
    def _(i):
        ACC[i] = jnp.zeros((U, U), F32)

    mine = pl.ds(pl.multiple_of(pos_of(0) * EL, EL), EL)
    EX[0:EL] = ET[mine]
    for r in range(1, 8):
        ecopy(r).wait_recv()

    ev = EX[...]
    sel = ev >= 0.0
    before = lax.broadcasted_iota(jnp.int32, (T, T), 0) < lax.broadcasted_iota(jnp.int32, (T, T), 1)
    cnt = _dot(sel.astype(F32).astype(BF), before.astype(F32).astype(BF))
    pos = jnp.where(sel, cnt, -1.0)
    POS[...] = pos

    @pl.loop(0, 8)
    def _(r):
        p = POS[pl.ds(pl.multiple_of(r * EL, EL), EL)]
        slot = lax.broadcasted_iota(jnp.int32, (C, T), 0).astype(F32)
        for e in range(EL):
            HT[r, e * C:(e + 1) * C, :] = jnp.where(jnp.broadcast_to(p[e:e + 1], (C, T)) == slot, 1.0, 0.0).astype(BF)

    fwd(0)
    own(2)

    ge = jnp.maximum(ev, 0.0)
    post = jnp.transpose(pos).astype(BF)
    gt = jnp.transpose(ge)
    hi = gt.astype(BF)
    rest = gt - hi.astype(F32)
    mid = rest.astype(BF)
    lo = (rest - mid.astype(F32)).astype(BF)

    @pl.loop(0, 8)
    def _(r):
        spread = jnp.where(lax.broadcasted_iota(jnp.int32, (8 * EL, S), 0)
                           == r * EL + lax.broadcasted_iota(jnp.int32, (8 * EL, S), 1) // C, 1.0, 0.0).astype(BF)
        slot = (lax.broadcasted_iota(jnp.int32, (T, S), 1) % C).astype(F32)
        hit = _dot(post, spread) == slot
        for k, part in enumerate((hi, mid, lo)):
            W[k * 8 + r] = jnp.where(hit, _dot(part, spread), 0.0).astype(BF)

    diag(0)
    fwd(1)
    own(3)
    arrived(0)
    diag(1)
    arrived(1)

    def gather(q):
        @pl.loop(0, 8)
        def _(r):
            rows = pl.ds(pl.multiple_of(r * C, C), C)
            for s in range(2):
                v = _dot(HT[r], X[(2 * q + s) * 8 + r])
                XIN[:, rows, s * U:(s + 1) * U] = v.astype(BF).reshape(EL, C, U)

    def tiles(n):
        wtload(n, 0).wait()
        wtload(n, 1).wait()

    @pl.loop(0, NQ - 1)
    def _(q):
        gather(q)

        @pl.loop(0, EL)
        def _(e):
            n = q * EL + e
            s = n % NWT
            tiles(n)
            xe = XIN[e]
            for m in range(2):
                for f in range(NF):
                    ACC[(e * 2 + m) * NF + f] += _dot(xe, WT[s, m, :, f * U:(f + 1) * U])
            for m in range(2):
                wtload(n + NWT, m).start()

            u = 2 * q + 2
            for at, step in ((2, lambda: fwd(u)), (6, lambda: diag(u)), (8, lambda: fwd(u + 1)), (12, lambda: diag(u + 1))):
                @pl.when(e == at)
                def _():
                    step()

            for at, k in ((2, 2), (8, 3)):
                @pl.when((e == at) & (u + k < NU))
                def _():
                    own(u + k)

        arrived(2 * q + 2)
        arrived(2 * q + 3)

    gather(NQ - 1)

    @pl.loop(0, NU)
    def _(u):
        sent(u)

    for r in range(1, 8):
        ecopy(r).wait_send()

    for n in range(NW2):
        w2load(n, 0).start()
        w2load(n, 1).start()

    @pl.loop(0, EL)
    def _(e):
        n = (NQ - 1) * EL + e
        s = n % NWT
        tiles(n)
        xe = XIN[e]
        for f in range(NF):
            a = ACC[e * 2 * NF + f] + _dot(xe, WT[s, 0, :, f * U:(f + 1) * U])
            b = ACC[(e * 2 + 1) * NF + f] + _dot(xe, WT[s, 1, :, f * U:(f + 1) * U])
            X[e * NF + f] = (jax.nn.silu(a) * b).astype(BF)

        @pl.when(n + NWT < NQ * EL)
        def _():
            for m in range(2):
                wtload(n + NWT, m).start()

    for r in (1, 2, 4):
        pl.semaphore_signal(ready, inc=1, device_id=did(r), device_id_type=MESH)

    R1 = 4 * NB
    R2 = R1 + 2 * NB
    YS = R2 + NB
    SS = YS + 8
    TT = SS + 12
    A = pl.ds(0, CW)
    B = pl.ds(CW, CW)

    def d2d(b):
        return pltpu.make_async_remote_copy(
            src_ref=ACC.at[pl.ds(YS + (b % 2) * 4, 4)], dst_ref=ACC.at[pl.ds(b * 4, 4)],
            send_sem=d2s.at[b], recv_sem=d2r.at[b], device_id=did(1), device_id_type=MESH)

    def hop1(b, k):
        src, dst, half, to = [(2, 0, A, 4), (3, 1, A, 4), (1, 0, B, 2), (3, 1, B, 2)][k]
        return pltpu.make_async_remote_copy(
            src_ref=ACC.at[SS + (b % 3) * 4 + src, :, half], dst_ref=ACC.at[R1 + b * 2 + dst, :, half],
            send_sem=p1s.at[b, k], recv_sem=p1r.at[b, k], device_id=did(to), device_id_type=MESH)

    def hop2(b, k):
        half, to = [(A, 2), (B, 4)][k]
        return pltpu.make_async_remote_copy(
            src_ref=ACC.at[TT + b % 2, :, half], dst_ref=ACC.at[R2 + b, :, half],
            send_sem=p2s.at[b, k], recv_sem=p2r.at[b, k], device_id=did(to), device_id_type=MESH)

    def combine(r):
        rows = slice(r * C, (r + 1) * C)
        o = OB[:, rows, :].reshape(S, 2 * CW)
        return _dot(W[r], o) + _dot(W[8 + r], o) + _dot(W[16 + r], o)

    @pl.loop(0, NB + 2)
    def _(b):
        @pl.when(b < NB)
        def _():
            @pl.loop(0, EL)
            def _(e):
                n = b * EL + e
                s = n % NW2
                w2load(n, 0).wait()
                w2load(n, 1).wait()
                h = jnp.concatenate([X[e * NF + f] for f in range(NF)], axis=1)
                OB[e] = _dot(h, W2T[s]).astype(BF)

                @pl.when(n + NW2 < NB * EL)
                def _():
                    w2load(n + NW2, 0).start()
                    w2load(n + NW2, 1).start()

            for i in range(4):
                ACC[YS + (b % 2) * 4 + i] = combine(2 * i + 1)

            @pl.when(b == 0)
            def _():
                pl.semaphore_wait(ready, 3)

            d2d(b).start()
            sb = SS + (b % 3) * 4
            for i in range(4):
                ACC[sb + i] = combine(2 * i)
            d2d(b).wait_recv()
            for i in (3, 2, 1, 0):
                ACC[sb + i] += ACC[b * 4 + i]
            for k in (1, 3, 0, 2):
                hop1(b, k).start()
            d2d(b).wait_send()

        c = b - 1

        @pl.when((c >= 0) & (c < NB))
        def _():
            sc = SS + (c % 3) * 4
            for k, i, half in ((1, 1, slice(0, CW)), (3, 2, slice(CW, 2 * CW))):
                hop1(c, k).wait_recv()
                ACC[TT + c % 2, :, half] = ACC[sc + i, :, half] + ACC[R1 + c * 2 + 1, :, half]
                hop2(c, (k - 1) // 2).start()
            for k in range(4):
                hop1(c, k).wait_send()

        f = b - 2

        @pl.when(f >= 0)
        def _():
            sf = SS + (f % 3) * 4
            hop1(f, 0).wait_recv()
            hop1(f, 2).wait_recv()
            for k, half in ((0, slice(0, CW)), (1, slice(CW, 2 * CW))):
                hop2(f, k).wait_recv()
                cols = pl.ds(pl.multiple_of(k * (D // 2) + f * CW, CW), CW)
                out_ref[:, cols] = (ACC[sf, :, half] + ACC[R1 + f * 2, :, half] + ACC[R2 + f, :, half]).astype(BF)
                hop2(f, k).wait_send()


def solution(mesh):
    tok = P(('data', 'outer', 'expert'), None)
    wsp = P(('outer', 'expert'), None, None)

    def local(x, wr, idx, w1, w3, w2):
        T, D = x.shape
        E = wr.shape[1]
        EL, _, FF = w1.shape
        K = idx.shape[1]
        C = 2 * T * K // E
        S = EL * C
        NU = D // U
        NB = D // (2 * CW)
        NF = FF // U
        any_ = pl.BlockSpec(memory_space=pl.ANY)
        dma = pltpu.SemaphoreType.DMA
        return pl.pallas_call(
            kernel,
            out_shape=jax.ShapeDtypeStruct((T, D), BF),
            in_specs=[any_] * 6,
            out_specs=pl.BlockSpec(memory_space=pltpu.VMEM),
            scratch_shapes=[
                pltpu.VMEM((NU * 8, T, U), BF),
                pltpu.VMEM((D, E), BF),
                pltpu.VMEM((T, K), jnp.int32),
                pltpu.VMEM((E, T), F32),
                pltpu.VMEM((8 * EL, T), F32),
                pltpu.VMEM((8 * EL, T), F32),
                pltpu.VMEM((8, S, T), BF),
                pltpu.VMEM((24, T, S), BF),
                pltpu.VMEM((EL, 8 * C, 2 * U), BF),
                pltpu.VMEM((EL * 2 * NF, 8 * C, U), F32),
                pltpu.VMEM((NWT, 2, 2 * U, FF), BF),
                pltpu.VMEM((NW2, FF, 2 * CW), BF),
                pltpu.VMEM((EL, 8 * C, 2 * CW), BF),
                dma((NU + 2,)), dma((NWT, 2)), dma((NW2, 2)),
                dma((8, NU)), dma((8, NU)), dma((8,)), dma((8,)),
                dma((NB,)), dma((NB,)), dma((NB, 4)), dma((NB, 4)), dma((NB, 2)), dma((NB, 2)),
                pltpu.SemaphoreType.REGULAR,
            ],
            compiler_params=pltpu.CompilerParams(collective_id=0, has_side_effects=True, vmem_limit_bytes=67043328),
        )(x, wr, idx, w1, w3, w2)

    return jax.shard_map(local, mesh=mesh, in_specs=(tok, P(None, None), tok, wsp, wsp, wsp), out_specs=tok, check_vma=False)
```

time: 903 us -> 169 us (0.19)
  blocking collectives: 559 us -> 0 us
  Pallas kernels: 0 us -> 164 us
  waiting for transfers between devices: 146 us -> 0 us
  matrix products: 102 us -> 0 us
  local copies, waits for them, and re-layouts: 74.4 us -> 3.79 us
  other arithmetic: 13.5 us -> 0 us
    all_to_all x3 -> x0, blocking collectives: 559 us -> none  [the longest x1 187 us: local(): buf = lax.all_to_all(buf, 'expert', 1, 1, tiled=True)]
    pallas_call x0 -> x1, Pallas kernels: none -> 164 us  [local(): pl.pallas_call(kernel, out_shape=jax.ShapeDtypeStruct((T, D), BF), in_spe...]
    all_to_all x1 -> x0, waiting for transfers between devices: 146 us -> none  [local(): o = lax.all_to_all(o, 'expert', 1, 1, tiled=True)]
    dot_general x6 -> x0, matrix products: 102 us -> none  [the longest x1 47.7 us: local(): jnp.einsum('ecf,efd->ecd', h, w2, preferred_element_type=jnp.float32)]
    all_to_all x3 -> x0, local copies, waits for them, and re-layouts: 17 us -> none  [the longest x1 8.04 us: local(): o = lax.all_to_all(o, 'expert', 1, 1, tiled=True)]
    convert_element_type x1 -> x0, local copies, waits for them, and re-layouts: 15.1 us -> none  [local(): jnp.einsum('tec,td->ecd', hit, x, preferred_element_type=jnp.float32)]
    reshape x2 -> x0, local copies, waits for them, and re-layouts: 10.6 us -> none  [the longest x1 8.02 us: local(): o = o.reshape(el, n, C, dm).transpose(1, 0, 2, 3).reshape(O, X, el * C, dm)]
    convert_element_type x2 -> x0, other arithmetic: 9.98 us -> none  [the longest x1 7.22 us: _split(): hi = w.astype(jnp.bfloat16)]
  transfers between devices with their start and end apart: 1 -> 0, of which waited for: 1 -> 0; matrix products, arithmetic and copies ran while one was open for 4% -> 0% of each run, Pallas kernels for 0% -> 0%
where the time goes in v1:
time: 169 us; the launch traced here: 168 us
  Pallas kernels  164 us (97%)
  local copies, waits for them, and re-layouts  3.79 us (2%)
    pallas_call x1, Pallas kernels, local(): pl.pallas_call(kernel, out_shape=jax.ShapeDtypeStruct((T, D), BF), in_spe...  164 us
    unnamed x2, local copies, waits for them, and re-layouts  3.79 us

profile of v1, /device:TPU:0, one launch (start us, length us, event | category | flops | bytes accessed | tf_op | source)
XLA Modules:
  0.0 168.0 jit_solution(13702711592583650467)
XLA Ops:
  0.0 1.5 copy.7.idx_hbm
  1.5 164.2 %shard_map.64 = bf16[256,2048]{1,0:T(8,128)(2,1)} custom-call(bf16[256,2048]{1,0:T(8,128)(2,1)} %x_hbm.1, bf16[2048,128]{1,0:T(8,128)(2,1)} %wr_hbm.1, s32[256,8]{1,0:T(8,128)} %copy.7.idx_hbm, bf16[16,2048,768]{2,1,0:T(8,128)(2,1)} %w1_hbm.1, bf16[16,2048,768]{2,1,0:T(8,128)(2,1)} %w3_hbm.1, bf16[16,768,2048]{2,1,0:T(8,128)(2,1)} %w2_hbm.1), custom_call_target="tpu_custom_call" | custom-call | tf_op jit(solution)/shard_map/pallas_call | solution.py:390
  165.7 2.3 %copy.9 = bf16[256,2048]{1,0:T(8,128)(2,1)} copy(bf16[256,2048]{1,0:T(8,128)(2,1)} %shard_map.64) | data formatting | bytes 2097152

commit v2 on v1

--- a/solution.py
+++ b/solution.py
@@ -12,8 +12,8 @@
 F32 = jnp.float32
 U = 256
 CW = 128
-NWT = 3
-NW2 = 4
+NWT = 6
+NW2 = 10
 
 
 def _dot(a, b):
@@ -27,7 +27,7 @@
     T, D = x_hbm.shape
     E = wr_hbm.shape[1]
     EL, _, FF = w1_hbm.shape
-    K = idx_hbm.shape[1]
+    K = idx_hbm.shape[0]
     C = 2 * T * K // E
     S = EL * C
     NU = D // U
@@ -69,10 +69,10 @@
         rows = pl.ds(pl.multiple_of(q * 2 * U, 2 * U), 2 * U)
         return pltpu.make_async_copy(src.at[e, rows, :], WT.at[s, m], wtsem.at[s, m])
 
-    def w2load(n, m):
+    def w2load(n):
         b, e, s = n // EL, n % EL, n % NW2
-        cols = pl.ds(pl.multiple_of(m * (D // 2) + b * CW, CW), CW)
-        return pltpu.make_async_copy(w2_hbm.at[e, :, cols], W2T.at[s, :, pl.ds(m * CW, CW)], w2sem.at[s, m])
+        cols = pl.ds(pl.multiple_of(b * 2 * CW, 2 * CW), 2 * CW)
+        return pltpu.make_async_copy(w2_hbm.at[e, :, cols], W2T.at[s], w2sem.at[s])
 
     H = T // 2
 
@@ -143,7 +143,7 @@
     for u in range(1, NU):
         logits = logits + _dot(X[u * 8], WR[u * U:(u + 1) * U])
     lane = lax.broadcasted_iota(jnp.int32, (T, E), 1)
-    ids = IDX[...]
+    ids = jnp.transpose(IDX[...].astype(F32)).astype(jnp.int32)
     chosen = lane == ids[:, 0:1]
     for j in range(1, K):
         chosen = chosen | (lane == ids[:, j:j + 1])
@@ -257,8 +257,7 @@
         ecopy(r).wait_send()
 
     for n in range(NW2):
-        w2load(n, 0).start()
-        w2load(n, 1).start()
+        w2load(n).start()
 
     @pl.loop(0, EL)
     def _(e):
@@ -317,15 +316,13 @@
             def _(e):
                 n = b * EL + e
                 s = n % NW2
-                w2load(n, 0).wait()
-                w2load(n, 1).wait()
+                w2load(n).wait()
                 h = jnp.concatenate([X[e * NF + f] for f in range(NF)], axis=1)
                 OB[e] = _dot(h, W2T[s]).astype(BF)
 
                 @pl.when(n + NW2 < NB * EL)
                 def _():
-                    w2load(n + NW2, 0).start()
-                    w2load(n + NW2, 1).start()
+                    w2load(n + NW2).start()
 
             for i in range(4):
                 ACC[YS + (b % 2) * 4 + i] = combine(2 * i + 1)
@@ -366,7 +363,7 @@
             hop1(f, 2).wait_recv()
             for k, half in ((0, slice(0, CW)), (1, slice(CW, 2 * CW))):
                 hop2(f, k).wait_recv()
-                cols = pl.ds(pl.multiple_of(k * (D // 2) + f * CW, CW), CW)
+                cols = pl.ds(pl.multiple_of(f * 2 * CW + k * CW, CW), CW)
                 out_ref[:, cols] = (ACC[sf, :, half] + ACC[R1 + f * 2, :, half] + ACC[R2 + f, :, half]).astype(BF)
                 hop2(f, k).wait_send()
 
@@ -395,7 +392,7 @@
             scratch_shapes=[
                 pltpu.VMEM((NU * 8, T, U), BF),
                 pltpu.VMEM((D, E), BF),
-                pltpu.VMEM((T, K), jnp.int32),
+                pltpu.VMEM((K, T), jnp.int32),
                 pltpu.VMEM((E, T), F32),
                 pltpu.VMEM((8 * EL, T), F32),
                 pltpu.VMEM((8 * EL, T), F32),
@@ -406,12 +403,12 @@
                 pltpu.VMEM((NWT, 2, 2 * U, FF), BF),
                 pltpu.VMEM((NW2, FF, 2 * CW), BF),
                 pltpu.VMEM((EL, 8 * C, 2 * CW), BF),
-                dma((NU + 2,)), dma((NWT, 2)), dma((NW2, 2)),
+                dma((NU + 2,)), dma((NWT, 2)), dma((NW2,)),
                 dma((8, NU)), dma((8, NU)), dma((8,)), dma((8,)),
                 dma((NB,)), dma((NB,)), dma((NB, 4)), dma((NB, 4)), dma((NB, 2)), dma((NB, 2)),
                 pltpu.SemaphoreType.REGULAR,
             ],
             compiler_params=pltpu.CompilerParams(collective_id=0, has_side_effects=True, vmem_limit_bytes=67043328),
-        )(x, wr, idx, w1, w3, w2)
+        )(x, wr, idx.T, w1, w3, w2)
 
     return jax.shard_map(local, mesh=mesh, in_specs=(tok, P(None, None), tok, wsp, wsp, wsp), out_specs=tok, check_vma=False)

time: 169 us -> 166 us (0.982)
    unnamed x2 -> x1, local copies, waits for them, and re-layouts: 3.79 us -> 2.3 us
where the time goes in v2:
time: 166 us
  Pallas kernels  164 us (99%)
  local copies, waits for them, and re-layouts  2.3 us (1%)
    pallas_call x1, Pallas kernels, local(): pl.pallas_call(kernel, out_shape=jax.ShapeDtypeStruct((T, D), BF), in_spe...  164 us

profile of v2, /device:TPU:0, one launch (start us, length us, event | category | flops | bytes accessed | tf_op | source)
XLA Modules:
  0.0 165.8 jit_solution(8150192302344637624)
XLA Ops:
  0.0 163.5 %shard_map.64 = bf16[256,2048]{1,0:T(8,128)(2,1)} custom-call(bf16[256,2048]{1,0:T(8,128)(2,1)} %x_hbm.1, bf16[2048,128]{1,0:T(8,128)(2,1)} %wr_hbm.1, s32[8,256]{1,0:T(8,128)} %bitcast.1, bf16[16,2048,768]{2,1,0:T(8,128)(2,1)} %w1_hbm.1, bf16[16,2048,768]{2,1,0:T(8,128)(2,1)} %w3_hbm.1, bf16[16,768,2048]{2,1,0:T(8,128)(2,1)} %w2_hbm.1), custom_call_target="tpu_custom_call" | custom-call | tf_op jit(solution)/shard_map/pallas_call | solution.py:387
  163.5 2.3 %copy.8 = bf16[256,2048]{1,0:T(8,128)(2,1)} copy(bf16[256,2048]{1,0:T(8,128)(2,1)} %shard_map.64) | data formatting | bytes 2097152

commit v3 on v2

--- a/solution.py
+++ b/solution.py
@@ -12,8 +12,8 @@
 F32 = jnp.float32
 U = 256
 CW = 128
-NWT = 6
-NW2 = 10
+NWT = 8
+UE = 4
 
 
 def _dot(a, b):
@@ -21,7 +21,7 @@
 
 
 def kernel(x_hbm, wr_hbm, idx_hbm, w1_hbm, w3_hbm, w2_hbm, out_ref,
-           X, WR, IDX, ET, EX, POS, HT, W, XIN, ACC, WT, W2T, OB,
+           X, WR, IDX, ET, EX, POS, HT, W, XIN, ACC, WT,
            xsem, wtsem, w2sem, dsend, drecv, esend, erecv,
            d2s, d2r, p1s, p1r, p2s, p2r, ready):
     T, D = x_hbm.shape
@@ -69,10 +69,22 @@
         rows = pl.ds(pl.multiple_of(q * 2 * U, 2 * U), 2 * U)
         return pltpu.make_async_copy(src.at[e, rows, :], WT.at[s, m], wtsem.at[s, m])
 
-    def w2load(n):
-        b, e, s = n // EL, n % EL, n % NW2
+    R = 2 * U
+
+    def w2load(b, e):
         cols = pl.ds(pl.multiple_of(b * 2 * CW, 2 * CW), 2 * CW)
-        return pltpu.make_async_copy(w2_hbm.at[e, :, cols], W2T.at[s], w2sem.at[s])
+        s, m = e // 2, e % 2
+        return (
+            pltpu.make_async_copy(w2_hbm.at[e, 0:R, cols], WT.at[s, m, :, 0:2 * CW], w2sem.at[e, 0]),
+            pltpu.make_async_copy(w2_hbm.at[e, R:FF, cols], WT.at[s, m, 0:FF - R, 2 * CW:4 * CW], w2sem.at[e, 1]))
+
+    def w2start(b, e):
+        for c in w2load(b, e):
+            c.start()
+
+    def w2tile(e):
+        s, m = e // 2, e % 2
+        return jnp.concatenate([WT[s, m, :, 0:2 * CW], WT[s, m, 0:FF - R, 2 * CW:4 * CW]], axis=0)
 
     H = T // 2
 
@@ -206,46 +218,63 @@
     arrived(1)
 
     def gather(q):
-        @pl.loop(0, 8)
-        def _(r):
-            rows = pl.ds(pl.multiple_of(r * C, C), C)
-            for s in range(2):
-                v = _dot(HT[r], X[(2 * q + s) * 8 + r])
-                XIN[:, rows, s * U:(s + 1) * U] = v.astype(BF).reshape(EL, C, U)
+        @pl.loop(0, 2)
+        def _(g):
+            for i in range(4):
+                r = g * 4 + i
+                rows = pl.ds(pl.multiple_of(r * C, C), C)
+                for s in range(2):
+                    v = _dot(HT[r], X[(2 * q + s) * 8 + r])
+                    XIN[:, rows, s * U:(s + 1) * U] = v.astype(BF).reshape(EL, C, U)
 
     def tiles(n):
-        wtload(n, 0).wait()
-        wtload(n, 1).wait()
+        for i in range(UE):
+            for m in range(2):
+                wtload(n + i, m).wait()
 
     @pl.loop(0, NQ - 1)
     def _(q):
+        u = 2 * q + 2
+        fwd(u)
+
+        @pl.when(u + 2 < NU)
+        def _():
+            own(u + 2)
+
         gather(q)
 
-        @pl.loop(0, EL)
-        def _(e):
-            n = q * EL + e
-            s = n % NWT
+        @pl.loop(0, EL // UE)
+        def _(g):
+            n = q * EL + g * UE
             tiles(n)
-            xe = XIN[e]
-            for m in range(2):
-                for f in range(NF):
-                    ACC[(e * 2 + m) * NF + f] += _dot(xe, WT[s, m, :, f * U:(f + 1) * U])
-            for m in range(2):
-                wtload(n + NWT, m).start()
-
-            u = 2 * q + 2
-            for at, step in ((2, lambda: fwd(u)), (6, lambda: diag(u)), (8, lambda: fwd(u + 1)), (12, lambda: diag(u + 1))):
-                @pl.when(e == at)
+            for i in range(UE):
+                e, s = g * UE + i, (n + i) % NWT
+                xe = XIN[e]
+                for m in range(2):
+                    for f in range(NF):
+                        ACC[(e * 2 + m) * NF + f] += _dot(xe, WT[s, m, :, f * U:(f + 1) * U])
+            for i in range(UE):
+                for m in range(2):
+                    wtload(n + NWT + i, m).start()
+
+            @pl.when(g == 0)
+            def _():
+                diag(u)
+
+            @pl.when(g == 1)
+            def _():
+                fwd(u + 1)
+
+                @pl.when(u + 3 < NU)
                 def _():
-                    step()
-
-            for at, k in ((2, 2), (8, 3)):
-                @pl.when((e == at) & (u + k < NU))
-                def _():
-                    own(u + k)
-
-        arrived(2 * q + 2)
-        arrived(2 * q + 3)
+                    own(u + 3)
+
+            @pl.when(g == 2)
+            def _():
+                diag(u + 1)
+
+        arrived(u)
+        arrived(u + 1)
 
     gather(NQ - 1)
 
@@ -256,24 +285,28 @@
     for r in range(1, 8):
         ecopy(r).wait_send()
 
-    for n in range(NW2):
-        w2load(n).start()
-
-    @pl.loop(0, EL)
-    def _(e):
-        n = (NQ - 1) * EL + e
-        s = n % NWT
+    @pl.loop(0, EL // UE)
+    def _(g):
+        n = (NQ - 1) * EL + g * UE
         tiles(n)
-        xe = XIN[e]
-        for f in range(NF):
-            a = ACC[e * 2 * NF + f] + _dot(xe, WT[s, 0, :, f * U:(f + 1) * U])
-            b = ACC[(e * 2 + 1) * NF + f] + _dot(xe, WT[s, 1, :, f * U:(f + 1) * U])
-            X[e * NF + f] = (jax.nn.silu(a) * b).astype(BF)
+        for i in range(UE):
+            e, s = g * UE + i, (n + i) % NWT
+            xe = XIN[e]
+            for f in range(NF):
+                a = ACC[e * 2 * NF + f] + _dot(xe, WT[s, 0, :, f * U:(f + 1) * U])
+                b = ACC[(e * 2 + 1) * NF + f] + _dot(xe, WT[s, 1, :, f * U:(f + 1) * U])
+                X[e * NF + f] = (jax.nn.silu(a) * b).astype(BF)
 
         @pl.when(n + NWT < NQ * EL)
         def _():
-            for m in range(2):
-                wtload(n + NWT, m).start()
+            for i in range(UE):
+                for m in range(2):
+                    wtload(n + NWT + i, m).start()
+
+        @pl.when(n + NWT >= NQ * EL)
+        def _():
+            for i in range(2 * UE):
+                w2start(0, (g - (EL // UE - 2)) * 2 * UE + i)
 
     for r in (1, 2, 4):
         pl.semaphore_signal(ready, inc=1, device_id=did(r), device_id_type=MESH)
@@ -305,24 +338,27 @@
 
     def combine(r):
         rows = slice(r * C, (r + 1) * C)
-        o = OB[:, rows, :].reshape(S, 2 * CW)
+        o = XIN[:, rows, 0:2 * CW].reshape(S, 2 * CW)
         return _dot(W[r], o) + _dot(W[8 + r], o) + _dot(W[16 + r], o)
 
     @pl.loop(0, NB + 2)
     def _(b):
         @pl.when(b < NB)
         def _():
-            @pl.loop(0, EL)
-            def _(e):
-                n = b * EL + e
-                s = n % NW2
-                w2load(n).wait()
-                h = jnp.concatenate([X[e * NF + f] for f in range(NF)], axis=1)
-                OB[e] = _dot(h, W2T[s]).astype(BF)
-
-                @pl.when(n + NW2 < NB * EL)
+            @pl.loop(0, EL // UE)
+            def _(g):
+                for i in range(UE):
+                    for c in w2load(b, g * UE + i):
+                        c.wait()
+                for i in range(UE):
+                    e = g * UE + i
+                    h = jnp.concatenate([X[e * NF + f] for f in range(NF)], axis=1)
+                    XIN[e, :, 0:2 * CW] = _dot(h, w2tile(e)).astype(BF)
+
+                @pl.when(b + 1 < NB)
                 def _():
-                    w2load(n + NW2).start()
+                    for i in range(UE):
+                        w2start(b + 1, g * UE + i)
 
             for i in range(4):
                 ACC[YS + (b % 2) * 4 + i] = combine(2 * i + 1)
@@ -401,9 +437,7 @@
                 pltpu.VMEM((EL, 8 * C, 2 * U), BF),
                 pltpu.VMEM((EL * 2 * NF, 8 * C, U), F32),
                 pltpu.VMEM((NWT, 2, 2 * U, FF), BF),
-                pltpu.VMEM((NW2, FF, 2 * CW), BF),
-                pltpu.VMEM((EL, 8 * C, 2 * CW), BF),
-                dma((NU + 2,)), dma((NWT, 2)), dma((NW2,)),
+                dma((NU + 2,)), dma((NWT, 2)), dma((EL, 2)),
                 dma((8, NU)), dma((8, NU)), dma((8,)), dma((8,)),
                 dma((NB,)), dma((NB,)), dma((NB, 4)), dma((NB, 4)), dma((NB, 2)), dma((NB, 2)),
                 pltpu.SemaphoreType.REGULAR,

time: 166 us -> 146 us (0.88)
  Pallas kernels: 164 us -> 143 us
    pallas_call x1, Pallas kernels: 164 us -> 143 us  [local(): pl.pallas_call(kernel, out_shape=jax.ShapeDtypeStruct((T, D), BF), in_spe...]
where the time goes in v3:
time: 146 us; the launch traced here: 145 us
  Pallas kernels  143 us (98%)
  local copies, waits for them, and re-layouts  2.3 us (2%)
    pallas_call x1, Pallas kernels, local(): pl.pallas_call(kernel, out_shape=jax.ShapeDtypeStruct((T, D), BF), in_spe...  143 us

profile of v3, /device:TPU:0, one launch (start us, length us, event | category | flops | bytes accessed | tf_op | source)
XLA Modules:
  0.0 145.4 jit_solution(13340579207721718388)
XLA Ops:
  0.0 143.1 %shard_map.64 = bf16[256,2048]{1,0:T(8,128)(2,1)} custom-call(bf16[256,2048]{1,0:T(8,128)(2,1)} %x_hbm.1, bf16[2048,128]{1,0:T(8,128)(2,1)} %wr_hbm.1, s32[8,256]{1,0:T(8,128)} %bitcast.1, bf16[16,2048,768]{2,1,0:T(8,128)(2,1)} %w1_hbm.1, bf16[16,2048,768]{2,1,0:T(8,128)(2,1)} %w3_hbm.1, bf16[16,768,2048]{2,1,0:T(8,128)(2,1)} %w2_hbm.1), custom_call_target="tpu_custom_call" | custom-call | tf_op jit(solution)/shard_map/pallas_call | solution.py:423
  143.1 2.3 %copy.8 = bf16[256,2048]{1,0:T(8,128)(2,1)} copy(bf16[256,2048]{1,0:T(8,128)(2,1)} %shard_map.64) | data formatting | bytes 2097152

commit v4 on v3

--- a/solution.py
+++ b/solution.py
@@ -12,7 +12,7 @@
 F32 = jnp.float32
 U = 256
 CW = 128
-NWT = 8
+NWT = 12
 UE = 4
 
 
@@ -20,10 +20,10 @@
     return jnp.dot(a, b, preferred_element_type=F32)
 
 
-def kernel(x_hbm, wr_hbm, idx_hbm, w1_hbm, w3_hbm, w2_hbm, out_ref,
-           X, WR, IDX, ET, EX, POS, HT, W, XIN, ACC, WT,
+def kernel(x_hbm, wr_hbm, idx_hbm, w1_hbm, w3_hbm, w2_hbm, out_hbm,
+           X, IDX, ET, EX, POS, HT, W, XIN, ACC, WT,
            xsem, wtsem, w2sem, dsend, drecv, esend, erecv,
-           d2s, d2r, p1s, p1r, p2s, p2r, ready):
+           d2s, d2r, p1s, p1r, p2s, p2r, osem, ready):
     T, D = x_hbm.shape
     E = wr_hbm.shape[1]
     EL, _, FF = w1_hbm.shape
@@ -60,8 +60,10 @@
     def xload(u):
         return pltpu.make_async_copy(x_hbm.at[:, pl.ds(u * U, U)], X.at[u * 8], xsem.at[u])
 
-    wrload = pltpu.make_async_copy(wr_hbm, WR, xsem.at[NU])
-    idxload = pltpu.make_async_copy(idx_hbm, IDX, xsem.at[NU + 1])
+    def wrload(u):
+        return pltpu.make_async_copy(wr_hbm.at[pl.ds(u * U, U)], XIN.at[u, :, 0:E], xsem.at[NU + u])
+
+    idxload = pltpu.make_async_copy(idx_hbm, IDX, xsem.at[2 * NU])
 
     def wtload(n, m):
         q, e, s = n // EL, n % EL, n % NWT
@@ -73,7 +75,7 @@
 
     def w2load(b, e):
         cols = pl.ds(pl.multiple_of(b * 2 * CW, 2 * CW), 2 * CW)
-        s, m = e // 2, e % 2
+        s, m = NWT - EL // 2 + e // 2, e % 2
         return (
             pltpu.make_async_copy(w2_hbm.at[e, 0:R, cols], WT.at[s, m, :, 0:2 * CW], w2sem.at[e, 0]),
             pltpu.make_async_copy(w2_hbm.at[e, R:FF, cols], WT.at[s, m, 0:FF - R, 2 * CW:4 * CW], w2sem.at[e, 1]))
@@ -83,7 +85,7 @@
             c.start()
 
     def w2tile(e):
-        s, m = e // 2, e % 2
+        s, m = NWT - EL // 2 + e // 2, e % 2
         return jnp.concatenate([WT[s, m, :, 0:2 * CW], WT[s, m, 0:FF - R, 2 * CW:4 * CW]], axis=0)
 
     H = T // 2
@@ -134,7 +136,8 @@
 
     for u in range(NU):
         xload(u).start()
-    wrload.start()
+    for u in range(NU):
+        wrload(u).start()
     idxload.start()
     for n in range(NWT):
         wtload(n, 0).start()
@@ -149,11 +152,12 @@
 
     for u in range(1, NU):
         xload(u).wait()
-    wrload.wait()
+    for u in range(NU):
+        wrload(u).wait()
     idxload.wait()
-    logits = _dot(X[0], WR[0:U])
+    logits = _dot(X[0], XIN[0, :, 0:E])
     for u in range(1, NU):
-        logits = logits + _dot(X[u * 8], WR[u * U:(u + 1) * U])
+        logits = logits + _dot(X[u * 8], XIN[u, :, 0:E])
     lane = lax.broadcasted_iota(jnp.int32, (T, E), 1)
     ids = jnp.transpose(IDX[...].astype(F32)).astype(jnp.int32)
     chosen = lane == ids[:, 0:1]
@@ -248,7 +252,7 @@
             n = q * EL + g * UE
             tiles(n)
             for i in range(UE):
-                e, s = g * UE + i, (n + i) % NWT
+                e, s = g * UE + i, n % NWT + i
                 xe = XIN[e]
                 for m in range(2):
                     for f in range(NF):
@@ -290,7 +294,7 @@
         n = (NQ - 1) * EL + g * UE
         tiles(n)
         for i in range(UE):
-            e, s = g * UE + i, (n + i) % NWT
+            e, s = g * UE + i, n % NWT + i
             xe = XIN[e]
             for f in range(NF):
                 a = ACC[e * 2 * NF + f] + _dot(xe, WT[s, 0, :, f * U:(f + 1) * U])
@@ -303,10 +307,10 @@
                 for m in range(2):
                     wtload(n + NWT + i, m).start()
 
-        @pl.when(n + NWT >= NQ * EL)
+        @pl.when((g == 1) | (g == 2))
         def _():
             for i in range(2 * UE):
-                w2start(0, (g - (EL // UE - 2)) * 2 * UE + i)
+                w2start(0, (g - 1) * 2 * UE + i)
 
     for r in (1, 2, 4):
         pl.semaphore_signal(ready, inc=1, device_id=did(r), device_id_type=MESH)
@@ -316,13 +320,19 @@
     YS = R2 + NB
     SS = YS + 8
     TT = SS + 12
+    OUT = EL * NF
+
+    def store(b):
+        cols = pl.ds(pl.multiple_of(b * 2 * CW, 2 * CW), 2 * CW)
+        return pltpu.make_async_copy(X.at[OUT + b], out_hbm.at[:, cols], osem.at[b])
+
     A = pl.ds(0, CW)
     B = pl.ds(CW, CW)
 
-    def d2d(b):
+    def d2d(b, i):
         return pltpu.make_async_remote_copy(
-            src_ref=ACC.at[pl.ds(YS + (b % 2) * 4, 4)], dst_ref=ACC.at[pl.ds(b * 4, 4)],
-            send_sem=d2s.at[b], recv_sem=d2r.at[b], device_id=did(1), device_id_type=MESH)
+            src_ref=ACC.at[YS + (b % 2) * 4 + i], dst_ref=ACC.at[b * 4 + i],
+            send_sem=d2s.at[b, i], recv_sem=d2r.at[b, i], device_id=did(1), device_id_type=MESH)
 
     def hop1(b, k):
         src, dst, half, to = [(2, 0, A, 4), (3, 1, A, 4), (1, 0, B, 2), (3, 1, B, 2)][k]
@@ -360,23 +370,33 @@
                     for i in range(UE):
                         w2start(b + 1, g * UE + i)
 
-            for i in range(4):
-                ACC[YS + (b % 2) * 4 + i] = combine(2 * i + 1)
-
             @pl.when(b == 0)
             def _():
                 pl.semaphore_wait(ready, 3)
 
-            d2d(b).start()
             sb = SS + (b % 3) * 4
+
+            def make(i):
+                ACC[YS + (b % 2) * 4 + i] = combine(2 * i + 1)
+                d2d(b, i).start()
+                ACC[sb + i] = combine(2 * i)
+
+            def total(i, hops):
+                d2d(b, i).wait_recv()
+                ACC[sb + i] += ACC[b * 4 + i]
+                for k in hops:
+                    hop1(b, k).start()
+
+            make(3)
+            make(2)
+            total(3, (1, 3))
+            make(1)
+            total(2, (0,))
+            make(0)
+            total(1, (2,))
+            total(0, ())
             for i in range(4):
-                ACC[sb + i] = combine(2 * i)
-            d2d(b).wait_recv()
-            for i in (3, 2, 1, 0):
-                ACC[sb + i] += ACC[b * 4 + i]
-            for k in (1, 3, 0, 2):
-                hop1(b, k).start()
-            d2d(b).wait_send()
+                d2d(b, i).wait_send()
 
         c = b - 1
 
@@ -399,9 +419,13 @@
             hop1(f, 2).wait_recv()
             for k, half in ((0, slice(0, CW)), (1, slice(CW, 2 * CW))):
                 hop2(f, k).wait_recv()
-                cols = pl.ds(pl.multiple_of(f * 2 * CW + k * CW, CW), CW)
-                out_ref[:, cols] = (ACC[sf, :, half] + ACC[R1 + f * 2, :, half] + ACC[R2 + f, :, half]).astype(BF)
+                X[OUT + f, :, half] = (ACC[sf, :, half] + ACC[R1 + f * 2, :, half] + ACC[R2 + f, :, half]).astype(BF)
                 hop2(f, k).wait_send()
+            store(f).start()
+
+    @pl.loop(0, NB)
+    def _(b):
+        store(b).wait()
 
 
 def solution(mesh):
@@ -424,10 +448,9 @@
             kernel,
             out_shape=jax.ShapeDtypeStruct((T, D), BF),
             in_specs=[any_] * 6,
-            out_specs=pl.BlockSpec(memory_space=pltpu.VMEM),
+            out_specs=any_,
             scratch_shapes=[
                 pltpu.VMEM((NU * 8, T, U), BF),
-                pltpu.VMEM((D, E), BF),
                 pltpu.VMEM((K, T), jnp.int32),
                 pltpu.VMEM((E, T), F32),
                 pltpu.VMEM((8 * EL, T), F32),
@@ -437,9 +460,9 @@
                 pltpu.VMEM((EL, 8 * C, 2 * U), BF),
                 pltpu.VMEM((EL * 2 * NF, 8 * C, U), F32),
                 pltpu.VMEM((NWT, 2, 2 * U, FF), BF),
-                dma((NU + 2,)), dma((NWT, 2)), dma((EL, 2)),
+                dma((2 * NU + 1,)), dma((NWT, 2)), dma((EL, 2)),
                 dma((8, NU)), dma((8, NU)), dma((8,)), dma((8,)),
-                dma((NB,)), dma((NB,)), dma((NB, 4)), dma((NB, 4)), dma((NB, 2)), dma((NB, 2)),
+                dma((NB, 4)), dma((NB, 4)), dma((NB, 4)), dma((NB, 4)), dma((NB, 2)), dma((NB, 2)), dma((NB,)),
                 pltpu.SemaphoreType.REGULAR,
             ],
             compiler_params=pltpu.CompilerParams(collective_id=0, has_side_effects=True, vmem_limit_bytes=67043328),

time: 146 us -> 147 us (level)
  Pallas kernels: 143 us -> 145 us
    pallas_call x1, Pallas kernels: 143 us -> 145 us  [local(): pl.pallas_call(kernel, out_shape=jax.ShapeDtypeStruct((T, D), BF), in_spe...]
where the time goes in v4:
time: 147 us
  Pallas kernels  145 us (99%)
  local copies, waits for them, and re-layouts  2.3 us (2%)
    pallas_call x1, Pallas kernels, local(): pl.pallas_call(kernel, out_shape=jax.ShapeDtypeStruct((T, D), BF), in_spe...  145 us

profile of v4, /device:TPU:0, one launch (start us, length us, event | category | flops | bytes accessed | tf_op | source)
XLA Modules:
  0.0 147.2 jit_solution(660758824282157929)
XLA Ops:
  0.0 144.8 %shard_map.64 = bf16[256,2048]{1,0:T(8,128)(2,1)} custom-call(bf16[256,2048]{1,0:T(8,128)(2,1)} %x_hbm.1, bf16[2048,128]{1,0:T(8,128)(2,1)} %wr_hbm.1, s32[8,256]{1,0:T(8,128)} %bitcast.1, bf16[16,2048,768]{2,1,0:T(8,128)(2,1)} %w1_hbm.1, bf16[16,2048,768]{2,1,0:T(8,128)(2,1)} %w3_hbm.1, bf16[16,768,2048]{2,1,0:T(8,128)(2,1)} %w2_hbm.1), custom_call_target="tpu_custom_call" | custom-call | tf_op jit(solution)/shard_map/pallas_call | solution.py:447
  144.8 2.3 %copy.8 = bf16[256,2048]{1,0:T(8,128)(2,1)} copy(bf16[256,2048]{1,0:T(8,128)(2,1)} %shard_map.64) | data formatting | bytes 2097152

commit v5 on v4

--- a/solution.py
+++ b/solution.py
@@ -12,8 +12,9 @@
 F32 = jnp.float32
 U = 256
 CW = 128
-NWT = 12
+UA = 8
 UE = 4
+NWT = 24
 
 
 def _dot(a, b):
@@ -31,7 +32,7 @@
     C = 2 * T * K // E
     S = EL * C
     NU = D // U
-    NQ = NU // 2
+    NG = EL // UA
     NB = D // (2 * CW)
     NF = FF // U
 
@@ -65,28 +66,38 @@
 
     idxload = pltpu.make_async_copy(idx_hbm, IDX, xsem.at[2 * NU])
 
-    def wtload(n, m):
-        q, e, s = n // EL, n % EL, n % NWT
+    def wtload(k, i, m):
         src = w1_hbm if m == 0 else w3_hbm
-        rows = pl.ds(pl.multiple_of(q * 2 * U, 2 * U), 2 * U)
-        return pltpu.make_async_copy(src.at[e, rows, :], WT.at[s, m], wtsem.at[s, m])
-
-    R = 2 * U
+        rows = pl.ds(pl.multiple_of((k // NG) * U, U), U)
+        s = (k % 3) * UA + i
+        return pltpu.make_async_copy(src.at[(k % NG) * UA + i, rows, :], WT.at[s, m], wtsem.at[s, m])
+
+    def wtstart(k):
+        for i in range(UA):
+            for m in range(2):
+                wtload(k, i, m).start()
+
+    def wtwait(k):
+        for i in range(UA):
+            for m in range(2):
+                wtload(k, i, m).wait()
+
+    def w2place(b, e):
+        return UA * (1 + b % 2) + e // 2, e % 2
 
     def w2load(b, e):
         cols = pl.ds(pl.multiple_of(b * 2 * CW, 2 * CW), 2 * CW)
-        s, m = NWT - EL // 2 + e // 2, e % 2
-        return (
-            pltpu.make_async_copy(w2_hbm.at[e, 0:R, cols], WT.at[s, m, :, 0:2 * CW], w2sem.at[e, 0]),
-            pltpu.make_async_copy(w2_hbm.at[e, R:FF, cols], WT.at[s, m, 0:FF - R, 2 * CW:4 * CW], w2sem.at[e, 1]))
+        s, m = w2place(b, e)
+        return [pltpu.make_async_copy(w2_hbm.at[e, pl.ds(f * U, U), cols], WT.at[s, m, :, f * U:(f + 1) * U],
+                                      w2sem.at[b % 2, e, f]) for f in range(NF)]
 
     def w2start(b, e):
         for c in w2load(b, e):
             c.start()
 
-    def w2tile(e):
-        s, m = NWT - EL // 2 + e // 2, e % 2
-        return jnp.concatenate([WT[s, m, :, 0:2 * CW], WT[s, m, 0:FF - R, 2 * CW:4 * CW]], axis=0)
+    def w2tile(b, e):
+        s, m = w2place(b, e)
+        return jnp.concatenate([WT[s, m, :, f * U:(f + 1) * U] for f in range(NF)], axis=0)
 
     H = T // 2
 
@@ -139,9 +150,8 @@
     for u in range(NU):
         wrload(u).start()
     idxload.start()
-    for n in range(NWT):
-        wtload(n, 0).start()
-        wtload(n, 1).start()
+    for k in range(3):
+        wtstart(k)
 
     barrier = pltpu.get_barrier_semaphore()
     for r in range(1, 8):
@@ -169,11 +179,9 @@
     ET[...] = jnp.transpose(jnp.where(chosen, g, -1.0))
     for r in range(1, 8):
         ecopy(r).start()
+    fwd(0)
     own(1)
-
-    @pl.loop(0, ACC.shape[0])
-    def _(i):
-        ACC[i] = jnp.zeros((U, U), F32)
+    own(2)
 
     mine = pl.ds(pl.multiple_of(pos_of(0) * EL, EL), EL)
     EX[0:EL] = ET[mine]
@@ -193,9 +201,6 @@
         slot = lax.broadcasted_iota(jnp.int32, (C, T), 0).astype(F32)
         for e in range(EL):
             HT[r, e * C:(e + 1) * C, :] = jnp.where(jnp.broadcast_to(p[e:e + 1], (C, T)) == slot, 1.0, 0.0).astype(BF)
-
-    fwd(0)
-    own(2)
 
     ge = jnp.maximum(ev, 0.0)
     post = jnp.transpose(pos).astype(BF)
@@ -205,82 +210,98 @@
     mid = rest.astype(BF)
     lo = (rest - mid.astype(F32)).astype(BF)
 
-    @pl.loop(0, 8)
-    def _(r):
-        spread = jnp.where(lax.broadcasted_iota(jnp.int32, (8 * EL, S), 0)
-                           == r * EL + lax.broadcasted_iota(jnp.int32, (8 * EL, S), 1) // C, 1.0, 0.0).astype(BF)
-        slot = (lax.broadcasted_iota(jnp.int32, (T, S), 1) % C).astype(F32)
-        hit = _dot(post, spread) == slot
-        for k, part in enumerate((hi, mid, lo)):
-            W[k * 8 + r] = jnp.where(hit, _dot(part, spread), 0.0).astype(BF)
-
-    diag(0)
-    fwd(1)
-    own(3)
-    arrived(0)
-    diag(1)
-    arrived(1)
-
-    def gather(q):
+    def weigh(r0):
+        @pl.loop(r0, r0 + 4)
+        def _(r):
+            spread = jnp.where(lax.broadcasted_iota(jnp.int32, (8 * EL, S), 0)
+                               == r * EL + lax.broadcasted_iota(jnp.int32, (8 * EL, S), 1) // C, 1.0, 0.0).astype(BF)
+            slot = (lax.broadcasted_iota(jnp.int32, (T, S), 1) % C).astype(F32)
+            hit = _dot(post, spread) == slot
+            for k, part in enumerate((hi, mid, lo)):
+                W[k * 8 + r] = jnp.where(hit, _dot(part, spread), 0.0).astype(BF)
+
+    def gather(u):
         @pl.loop(0, 2)
         def _(g):
             for i in range(4):
                 r = g * 4 + i
                 rows = pl.ds(pl.multiple_of(r * C, C), C)
-                for s in range(2):
-                    v = _dot(HT[r], X[(2 * q + s) * 8 + r])
-                    XIN[:, rows, s * U:(s + 1) * U] = v.astype(BF).reshape(EL, C, U)
-
-    def tiles(n):
-        for i in range(UE):
-            for m in range(2):
-                wtload(n + i, m).wait()
-
-    @pl.loop(0, NQ - 1)
-    def _(q):
-        u = 2 * q + 2
-        fwd(u)
-
-        @pl.when(u + 2 < NU)
+                XIN[:, rows, :] = _dot(HT[r], X[u * 8 + r]).astype(BF).reshape(EL, C, U)
+
+    def experts(k, put):
+        wtwait(k)
+        for i in range(UA):
+            e, s = (k % NG) * UA + i, (k % 3) * UA + i
+            xe = XIN[e]
+            for f in range(NF):
+                put(e, f, _dot(xe, WT[s, 0, :, f * U:(f + 1) * U]), _dot(xe, WT[s, 1, :, f * U:(f + 1) * U]))
+
+    def first(e, f, a, b):
+        ACC[e * 2 * NF + f] = a
+        ACC[(e * 2 + 1) * NF + f] = b
+
+    def middle(e, f, a, b):
+        ACC[e * 2 * NF + f] += a
+        ACC[(e * 2 + 1) * NF + f] += b
+
+    def last(e, f, a, b):
+        a = ACC[e * 2 * NF + f] + a
+        b = ACC[(e * 2 + 1) * NF + f] + b
+        X[e * NF + f] = (jax.nn.silu(a) * b).astype(BF)
+
+    weigh(0)
+    fwd(1)
+    own(3)
+    diag(0)
+    arrived(0)
+    gather(0)
+
+    @pl.loop(0, NG)
+    def _(g):
+        experts(g, first)
+        wtstart(g + 3)
+
+        @pl.when(g == 0)
         def _():
-            own(u + 2)
-
-        gather(q)
-
-        @pl.loop(0, EL // UE)
+            fwd(2)
+            own(4)
+
+    diag(1)
+    weigh(4)
+
+    @pl.loop(1, NU - 1)
+    def _(u):
+        arrived(u)
+        gather(u)
+
+        @pl.loop(0, NG)
         def _(g):
-            n = q * EL + g * UE
-            tiles(n)
-            for i in range(UE):
-                e, s = g * UE + i, n % NWT + i
-                xe = XIN[e]
-                for m in range(2):
-                    for f in range(NF):
-                        ACC[(e * 2 + m) * NF + f] += _dot(xe, WT[s, m, :, f * U:(f + 1) * U])
-            for i in range(UE):
-                for m in range(2):
-                    wtload(n + NWT + i, m).start()
+            k = u * NG + g
+            experts(k, middle)
+
+            @pl.when(k + 3 < NU * NG)
+            def _():
+                wtstart(k + 3)
+
+            @pl.when(k + 3 == NU * NG)
+            def _():
+                for e in range(EL):
+                    w2start(0, e)
 
             @pl.when(g == 0)
             def _():
-                diag(u)
-
-            @pl.when(g == 1)
-            def _():
-                fwd(u + 1)
-
-                @pl.when(u + 3 < NU)
+                diag(u + 1)
+
+                @pl.when(u + 2 < NU)
                 def _():
-                    own(u + 3)
-
-            @pl.when(g == 2)
-            def _():
-                diag(u + 1)
-
-        arrived(u)
-        arrived(u + 1)
-
-    gather(NQ - 1)
+                    fwd(u + 2)
+
+                @pl.when(u + 4 < NU)
+                def _():
+                    own(u + 4)
+
+    arrived(NU - 1)
+    gather(NU - 1)
 
     @pl.loop(0, NU)
     def _(u):
@@ -289,28 +310,14 @@
     for r in range(1, 8):
         ecopy(r).wait_send()
 
-    @pl.loop(0, EL // UE)
+    @pl.loop(0, NG)
     def _(g):
-        n = (NQ - 1) * EL + g * UE
-        tiles(n)
-        for i in range(UE):
-            e, s = g * UE + i, n % NWT + i
-            xe = XIN[e]
-            for f in range(NF):
-                a = ACC[e * 2 * NF + f] + _dot(xe, WT[s, 0, :, f * U:(f + 1) * U])
-                b = ACC[(e * 2 + 1) * NF + f] + _dot(xe, WT[s, 1, :, f * U:(f + 1) * U])
-                X[e * NF + f] = (jax.nn.silu(a) * b).astype(BF)
-
-        @pl.when(n + NWT < NQ * EL)
+        experts((NU - 1) * NG + g, last)
+
+        @pl.when(g == 0)
         def _():
-            for i in range(UE):
-                for m in range(2):
-                    wtload(n + NWT + i, m).start()
-
-        @pl.when((g == 1) | (g == 2))
-        def _():
-            for i in range(2 * UE):
-                w2start(0, (g - 1) * 2 * UE + i)
+            for e in range(EL):
+                w2start(1, e)
 
     for r in (1, 2, 4):
         pl.semaphore_signal(ready, inc=1, device_id=did(r), device_id_type=MESH)
@@ -319,7 +326,7 @@
     R2 = R1 + 2 * NB
     YS = R2 + NB
     SS = YS + 8
-    TT = SS + 12
+    TT = SS + 16
     OUT = EL * NF
 
     def store(b):
@@ -337,21 +344,21 @@
     def hop1(b, k):
         src, dst, half, to = [(2, 0, A, 4), (3, 1, A, 4), (1, 0, B, 2), (3, 1, B, 2)][k]
         return pltpu.make_async_remote_copy(
-            src_ref=ACC.at[SS + (b % 3) * 4 + src, :, half], dst_ref=ACC.at[R1 + b * 2 + dst, :, half],
+            src_ref=ACC.at[SS + (b % 4) * 4 + src, :, half], dst_ref=ACC.at[R1 + b * 2 + dst, :, half],
             send_sem=p1s.at[b, k], recv_sem=p1r.at[b, k], device_id=did(to), device_id_type=MESH)
 
     def hop2(b, k):
         half, to = [(A, 2), (B, 4)][k]
         return pltpu.make_async_remote_copy(
-            src_ref=ACC.at[TT + b % 2, :, half], dst_ref=ACC.at[R2 + b, :, half],
+            src_ref=ACC.at[TT + b % 4, :, half], dst_ref=ACC.at[R2 + b, :, half],
             send_sem=p2s.at[b, k], recv_sem=p2r.at[b, k], device_id=did(to), device_id_type=MESH)
 
     def combine(r):
         rows = slice(r * C, (r + 1) * C)
-        o = XIN[:, rows, 0:2 * CW].reshape(S, 2 * CW)
+        o = XIN[:, rows, :].reshape(S, 2 * CW)
         return _dot(W[r], o) + _dot(W[8 + r], o) + _dot(W[16 + r], o)
 
-    @pl.loop(0, NB + 2)
+    @pl.loop(0, NB + 3)
     def _(b):
         @pl.when(b < NB)
         def _():
@@ -363,18 +370,18 @@
                 for i in range(UE):
                     e = g * UE + i
                     h = jnp.concatenate([X[e * NF + f] for f in range(NF)], axis=1)
-                    XIN[e, :, 0:2 * CW] = _dot(h, w2tile(e)).astype(BF)
-
-                @pl.when(b + 1 < NB)
+                    XIN[e] = _dot(h, w2tile(b, e)).astype(BF)
+
+                @pl.when(b + 2 < NB)
                 def _():
                     for i in range(UE):
-                        w2start(b + 1, g * UE + i)
+                        w2start(b + 2, g * UE + i)
 
             @pl.when(b == 0)
             def _():
                 pl.semaphore_wait(ready, 3)
 
-            sb = SS + (b % 3) * 4
+            sb = SS + (b % 4) * 4
 
             def make(i):
                 ACC[YS + (b % 2) * 4 + i] = combine(2 * i + 1)
@@ -402,19 +409,19 @@
 
         @pl.when((c >= 0) & (c < NB))
         def _():
-            sc = SS + (c % 3) * 4
+            sc = SS + (c % 4) * 4
             for k, i, half in ((1, 1, slice(0, CW)), (3, 2, slice(CW, 2 * CW))):
                 hop1(c, k).wait_recv()
-                ACC[TT + c % 2, :, half] = ACC[sc + i, :, half] + ACC[R1 + c * 2 + 1, :, half]
+                ACC[TT + c % 4, :, half] = ACC[sc + i, :, half] + ACC[R1 + c * 2 + 1, :, half]
                 hop2(c, (k - 1) // 2).start()
-            for k in range(4):
-                hop1(c, k).wait_send()
-
-        f = b - 2
+
+        f = b - 3
 
         @pl.when(f >= 0)
         def _():
-            sf = SS + (f % 3) * 4
+            sf = SS + (f % 4) * 4
+            for k in range(4):
+                hop1(f, k).wait_send()
             hop1(f, 0).wait_recv()
             hop1(f, 2).wait_recv()
             for k, half in ((0, slice(0, CW)), (1, slice(CW, 2 * CW))):
@@ -457,10 +464,10 @@
                 pltpu.VMEM((8 * EL, T), F32),
                 pltpu.VMEM((8, S, T), BF),
                 pltpu.VMEM((24, T, S), BF),
-                pltpu.VMEM((EL, 8 * C, 2 * U), BF),
+                pltpu.VMEM((EL, 8 * C, U), BF),
                 pltpu.VMEM((EL * 2 * NF, 8 * C, U), F32),
-                pltpu.VMEM((NWT, 2, 2 * U, FF), BF),
-                dma((2 * NU + 1,)), dma((NWT, 2)), dma((EL, 2)),
+                pltpu.VMEM((NWT, 2, U, FF), BF),
+                dma((2 * NU + 1,)), dma((NWT, 2)), dma((2, EL, NF)),
                 dma((8, NU)), dma((8, NU)), dma((8,)), dma((8,)),
                 dma((NB, 4)), dma((NB, 4)), dma((NB, 4)), dma((NB, 4)), dma((NB, 2)), dma((NB, 2)), dma((NB,)),
                 pltpu.SemaphoreType.REGULAR,

time: 147 us -> 149 us (1.014)
  Pallas kernels: 145 us -> 147 us
    pallas_call x1, Pallas kernels: 145 us -> 147 us  [local(): pl.pallas_call(kernel, out_shape=jax.ShapeDtypeStruct((T, D), BF), in_spe...]
where the time goes in v5:
time: 149 us
  Pallas kernels  147 us (99%)
  local copies, waits for them, and re-layouts  2.3 us (2%)
    pallas_call x1, Pallas kernels, local(): pl.pallas_call(kernel, out_shape=jax.ShapeDtypeStruct((T, D), BF), in_spe...  147 us

profile of v5, /device:TPU:0, one launch (start us, length us, event | category | flops | bytes accessed | tf_op | source)
XLA Modules:
  0.0 149.3 jit_solution(6751901095687627896)
XLA Ops:
  0.0 147.0 %shard_map.64 = bf16[256,2048]{1,0:T(8,128)(2,1)} custom-call(bf16[256,2048]{1,0:T(8,128)(2,1)} %x_hbm.1, bf16[2048,128]{1,0:T(8,128)(2,1)} %wr_hbm.1, s32[8,256]{1,0:T(8,128)} %bitcast.1, bf16[16,2048,768]{2,1,0:T(8,128)(2,1)} %w1_hbm.1, bf16[16,2048,768]{2,1,0:T(8,128)(2,1)} %w3_hbm.1, bf16[16,768,2048]{2,1,0:T(8,128)(2,1)} %w2_hbm.1), custom_call_target="tpu_custom_call" | custom-call | tf_op jit(solution)/shard_map/pallas_call | solution.py:454
  147.0 2.3 %copy.8 = bf16[256,2048]{1,0:T(8,128)(2,1)} copy(bf16[256,2048]{1,0:T(8,128)(2,1)} %shard_map.64) | data formatting | bytes 2097152

commit v6 on v4

--- a/solution.py
+++ b/solution.py
@@ -175,6 +175,8 @@
     def _(i):
         ACC[i] = jnp.zeros((U, U), F32)
 
+    fwd(0)
+
     mine = pl.ds(pl.multiple_of(pos_of(0) * EL, EL), EL)
     EX[0:EL] = ET[mine]
     for r in range(1, 8):
@@ -193,9 +195,6 @@
         slot = lax.broadcasted_iota(jnp.int32, (C, T), 0).astype(F32)
         for e in range(EL):
             HT[r, e * C:(e + 1) * C, :] = jnp.where(jnp.broadcast_to(p[e:e + 1], (C, T)) == slot, 1.0, 0.0).astype(BF)
-
-    fwd(0)
-    own(2)
 
     ge = jnp.maximum(ev, 0.0)
     post = jnp.transpose(pos).astype(BF)
@@ -205,8 +204,7 @@
     mid = rest.astype(BF)
     lo = (rest - mid.astype(F32)).astype(BF)
 
-    @pl.loop(0, 8)
-    def _(r):
+    def weigh(r):
         spread = jnp.where(lax.broadcasted_iota(jnp.int32, (8 * EL, S), 0)
                            == r * EL + lax.broadcasted_iota(jnp.int32, (8 * EL, S), 1) // C, 1.0, 0.0).astype(BF)
         slot = (lax.broadcasted_iota(jnp.int32, (T, S), 1) % C).astype(F32)
@@ -214,22 +212,21 @@
         for k, part in enumerate((hi, mid, lo)):
             W[k * 8 + r] = jnp.where(hit, _dot(part, spread), 0.0).astype(BF)
 
+    pl.loop(0, 4)(weigh)
+    fwd(1)
+    own(2)
+    own(3)
+    pl.loop(4, 8)(weigh)
     diag(0)
-    fwd(1)
-    own(3)
+    diag(1)
     arrived(0)
-    diag(1)
     arrived(1)
 
     def gather(q):
-        @pl.loop(0, 2)
-        def _(g):
-            for i in range(4):
-                r = g * 4 + i
-                rows = pl.ds(pl.multiple_of(r * C, C), C)
-                for s in range(2):
-                    v = _dot(HT[r], X[(2 * q + s) * 8 + r])
-                    XIN[:, rows, s * U:(s + 1) * U] = v.astype(BF).reshape(EL, C, U)
+        for r in range(8):
+            for s in range(2):
+                v = _dot(HT[r], X[(2 * q + s) * 8 + r])
+                XIN[:, r * C:(r + 1) * C, s * U:(s + 1) * U] = v.astype(BF).reshape(EL, C, U)
 
     def tiles(n):
         for i in range(UE):
@@ -239,13 +236,13 @@
     @pl.loop(0, NQ - 1)
     def _(q):
         u = 2 * q + 2
+        gather(q)
         fwd(u)
 
         @pl.when(u + 2 < NU)
         def _():
             own(u + 2)
 
-        gather(q)
 
         @pl.loop(0, EL // UE)
         def _(g):
@@ -261,22 +258,16 @@
                 for m in range(2):
                     wtload(n + NWT + i, m).start()
 
-            @pl.when(g == 0)
+            @pl.when(g == 1)
             def _():
                 diag(u)
-
-            @pl.when(g == 1)
-            def _():
                 fwd(u + 1)
 
                 @pl.when(u + 3 < NU)
                 def _():
                     own(u + 3)
 
-            @pl.when(g == 2)
-            def _():
-                diag(u + 1)
-
+        diag(u + 1)
         arrived(u)
         arrived(u + 1)
 
@@ -319,7 +310,7 @@
     R2 = R1 + 2 * NB
     YS = R2 + NB
     SS = YS + 8
-    TT = SS + 12
+    TT = SS + 16
     OUT = EL * NF
 
     def store(b):
@@ -337,13 +328,13 @@
     def hop1(b, k):
         src, dst, half, to = [(2, 0, A, 4), (3, 1, A, 4), (1, 0, B, 2), (3, 1, B, 2)][k]
         return pltpu.make_async_remote_copy(
-            src_ref=ACC.at[SS + (b % 3) * 4 + src, :, half], dst_ref=ACC.at[R1 + b * 2 + dst, :, half],
+            src_ref=ACC.at[SS + (b % 4) * 4 + src, :, half], dst_ref=ACC.at[R1 + b * 2 + dst, :, half],
             send_sem=p1s.at[b, k], recv_sem=p1r.at[b, k], device_id=did(to), device_id_type=MESH)
 
     def hop2(b, k):
         half, to = [(A, 2), (B, 4)][k]
         return pltpu.make_async_remote_copy(
-            src_ref=ACC.at[TT + b % 2, :, half], dst_ref=ACC.at[R2 + b, :, half],
+            src_ref=ACC.at[TT + b % 4, :, half], dst_ref=ACC.at[R2 + b, :, half],
             send_sem=p2s.at[b, k], recv_sem=p2r.at[b, k], device_id=did(to), device_id_type=MESH)
 
     def combine(r):
@@ -351,30 +342,27 @@
         o = XIN[:, rows, 0:2 * CW].reshape(S, 2 * CW)
         return _dot(W[r], o) + _dot(W[8 + r], o) + _dot(W[16 + r], o)
 
-    @pl.loop(0, NB + 2)
+    @pl.loop(0, NB + 3)
     def _(b):
         @pl.when(b < NB)
         def _():
-            @pl.loop(0, EL // UE)
-            def _(g):
-                for i in range(UE):
-                    for c in w2load(b, g * UE + i):
-                        c.wait()
-                for i in range(UE):
-                    e = g * UE + i
-                    h = jnp.concatenate([X[e * NF + f] for f in range(NF)], axis=1)
-                    XIN[e, :, 0:2 * CW] = _dot(h, w2tile(e)).astype(BF)
-
-                @pl.when(b + 1 < NB)
-                def _():
-                    for i in range(UE):
-                        w2start(b + 1, g * UE + i)
+            for e in range(EL):
+                for c in w2load(b, e):
+                    c.wait()
+            for e in range(EL):
+                h = jnp.concatenate([X[e * NF + f] for f in range(NF)], axis=1)
+                XIN[e, :, 0:2 * CW] = _dot(h, w2tile(e)).astype(BF)
+
+            @pl.when(b + 1 < NB)
+            def _():
+                for e in range(EL):
+                    w2start(b + 1, e)
 
             @pl.when(b == 0)
             def _():
                 pl.semaphore_wait(ready, 3)
 
-            sb = SS + (b % 3) * 4
+            sb = SS + (b % 4) * 4
 
             def make(i):
                 ACC[YS + (b % 2) * 4 + i] = combine(2 * i + 1)
@@ -402,19 +390,19 @@
 
         @pl.when((c >= 0) & (c < NB))
         def _():
-            sc = SS + (c % 3) * 4
+            sc = SS + (c % 4) * 4
             for k, i, half in ((1, 1, slice(0, CW)), (3, 2, slice(CW, 2 * CW))):
                 hop1(c, k).wait_recv()
-                ACC[TT + c % 2, :, half] = ACC[sc + i, :, half] + ACC[R1 + c * 2 + 1, :, half]
+                ACC[TT + c % 4, :, half] = ACC[sc + i, :, half] + ACC[R1 + c * 2 + 1, :, half]
                 hop2(c, (k - 1) // 2).start()
+
+        f = b - 3
+
+        @pl.when(f >= 0)
+        def _():
+            sf = SS + (f % 4) * 4
             for k in range(4):
-                hop1(c, k).wait_send()
-
-        f = b - 2
-
-        @pl.when(f >= 0)
-        def _():
-            sf = SS + (f % 3) * 4
+                hop1(f, k).wait_send()
             hop1(f, 0).wait_recv()
             hop1(f, 2).wait_recv()
             for k, half in ((0, slice(0, CW)), (1, slice(CW, 2 * CW))):

time: 147 us -> 143 us (0.973)
  Pallas kernels: 145 us -> 140 us
    pallas_call x1, Pallas kernels: 145 us -> 140 us  [local(): pl.pallas_call(kernel, out_shape=jax.ShapeDtypeStruct((T, D), BF), in_spe...]
where the time goes in v6:
time: 143 us
  Pallas kernels  140 us (98%)
  local copies, waits for them, and re-layouts  2.3 us (2%)
    pallas_call x1, Pallas kernels, local(): pl.pallas_call(kernel, out_shape=jax.ShapeDtypeStruct((T, D), BF), in_spe...  140 us

profile of v6, /device:TPU:0, one launch (start us, length us, event | category | flops | bytes accessed | tf_op | source)
XLA Modules:
  0.0 142.7 jit_solution(2146085447317070341)
XLA Ops:
  0.0 140.4 %shard_map.64 = bf16[256,2048]{1,0:T(8,128)(2,1)} custom-call(bf16[256,2048]{1,0:T(8,128)(2,1)} %x_hbm.1, bf16[2048,128]{1,0:T(8,128)(2,1)} %wr_hbm.1, s32[8,256]{1,0:T(8,128)} %bitcast.1, bf16[16,2048,768]{2,1,0:T(8,128)(2,1)} %w1_hbm.1, bf16[16,2048,768]{2,1,0:T(8,128)(2,1)} %w3_hbm.1, bf16[16,768,2048]{2,1,0:T(8,128)(2,1)} %w2_hbm.1), custom_call_target="tpu_custom_call" | custom-call | tf_op jit(solution)/shard_map/pallas_call | solution.py:435
  140.4 2.3 %copy.8 = bf16[256,2048]{1,0:T(8,128)(2,1)} copy(bf16[256,2048]{1,0:T(8,128)(2,1)} %shard_map.64) | data formatting | bytes 2097152

commit v7 on v6

--- a/solution.py
+++ b/solution.py
@@ -73,20 +73,25 @@
 
     R = 2 * U
 
+    def w2place(b, e):
+        p = b % 2
+        s, m = NWT - EL // 2 + e // 2, e % 2
+        return ((s, m, slice(None), pl.ds(pl.multiple_of(p * 4 * CW, 4 * CW), 2 * CW)),
+                (s, m, pl.ds(pl.multiple_of(p * (FF - R), FF - R), FF - R), slice(2 * CW, 4 * CW)))
+
     def w2load(b, e):
         cols = pl.ds(pl.multiple_of(b * 2 * CW, 2 * CW), 2 * CW)
-        s, m = NWT - EL // 2 + e // 2, e % 2
-        return (
-            pltpu.make_async_copy(w2_hbm.at[e, 0:R, cols], WT.at[s, m, :, 0:2 * CW], w2sem.at[e, 0]),
-            pltpu.make_async_copy(w2_hbm.at[e, R:FF, cols], WT.at[s, m, 0:FF - R, 2 * CW:4 * CW], w2sem.at[e, 1]))
+        top, low = w2place(b, e)
+        return (pltpu.make_async_copy(w2_hbm.at[e, 0:R, cols], WT.at[top], w2sem.at[b % 2, e, 0]),
+                pltpu.make_async_copy(w2_hbm.at[e, R:FF, cols], WT.at[low], w2sem.at[b % 2, e, 1]))
 
     def w2start(b, e):
         for c in w2load(b, e):
             c.start()
 
-    def w2tile(e):
-        s, m = NWT - EL // 2 + e // 2, e % 2
-        return jnp.concatenate([WT[s, m, :, 0:2 * CW], WT[s, m, 0:FF - R, 2 * CW:4 * CW]], axis=0)
+    def w2tile(b, e):
+        top, low = w2place(b, e)
+        return jnp.concatenate([WT[top], WT[low]], axis=0)
 
     H = T // 2
 
@@ -139,9 +144,6 @@
     for u in range(NU):
         wrload(u).start()
     idxload.start()
-    for n in range(NWT):
-        wtload(n, 0).start()
-        wtload(n, 1).start()
 
     barrier = pltpu.get_barrier_semaphore()
     for r in range(1, 8):
@@ -176,6 +178,9 @@
         ACC[i] = jnp.zeros((U, U), F32)
 
     fwd(0)
+    for n in range(NWT):
+        wtload(n, 0).start()
+        wtload(n, 1).start()
 
     mine = pl.ds(pl.multiple_of(pos_of(0) * EL, EL), EL)
     EX[0:EL] = ET[mine]
@@ -254,10 +259,6 @@
                 for m in range(2):
                     for f in range(NF):
                         ACC[(e * 2 + m) * NF + f] += _dot(xe, WT[s, m, :, f * U:(f + 1) * U])
-            for i in range(UE):
-                for m in range(2):
-                    wtload(n + NWT + i, m).start()
-
             @pl.when(g == 1)
             def _():
                 diag(u)
@@ -266,6 +267,10 @@
                 @pl.when(u + 3 < NU)
                 def _():
                     own(u + 3)
+
+            for i in range(UE):
+                for m in range(2):
+                    wtload(n + NWT + i, m).start()
 
         diag(u + 1)
         arrived(u)
@@ -302,6 +307,7 @@
         def _():
             for i in range(2 * UE):
                 w2start(0, (g - 1) * 2 * UE + i)
+                w2start(1, (g - 1) * 2 * UE + i)
 
     for r in (1, 2, 4):
         pl.semaphore_signal(ready, inc=1, device_id=did(r), device_id_type=MESH)
@@ -351,12 +357,7 @@
                     c.wait()
             for e in range(EL):
                 h = jnp.concatenate([X[e * NF + f] for f in range(NF)], axis=1)
-                XIN[e, :, 0:2 * CW] = _dot(h, w2tile(e)).astype(BF)
-
-            @pl.when(b + 1 < NB)
-            def _():
-                for e in range(EL):
-                    w2start(b + 1, e)
+                XIN[e, :, 0:2 * CW] = _dot(h, w2tile(b, e)).astype(BF)
 
             @pl.when(b == 0)
             def _():
@@ -385,6 +386,11 @@
             total(0, ())
             for i in range(4):
                 d2d(b, i).wait_send()
+
+            @pl.when(b + 2 < NB)
+            def _():
+                for e in range(EL):
+                    w2start(b + 2, e)
 
         c = b - 1
 
@@ -448,7 +454,7 @@
                 pltpu.VMEM((EL, 8 * C, 2 * U), BF),
                 pltpu.VMEM((EL * 2 * NF, 8 * C, U), F32),
                 pltpu.VMEM((NWT, 2, 2 * U, FF), BF),
-                dma((2 * NU + 1,)), dma((NWT, 2)), dma((EL, 2)),
+                dma((2 * NU + 1,)), dma((NWT, 2)), dma((2, EL, 2)),
                 dma((8, NU)), dma((8, NU)), dma((8,)), dma((8,)),
                 dma((NB, 4)), dma((NB, 4)), dma((NB, 4)), dma((NB, 4)), dma((NB, 2)), dma((NB, 2)), dma((NB,)),
                 pltpu.SemaphoreType.REGULAR,

time: 143 us -> 141 us (0.986)
    pallas_call x1, Pallas kernels: 140 us -> 139 us  [local(): pl.pallas_call(kernel, out_shape=jax.ShapeDtypeStruct((T, D), BF), in_spe...]
where the time goes in v7:
time: 141 us
  Pallas kernels  139 us (99%)
  local copies, waits for them, and re-layouts  2.3 us (2%)
    pallas_call x1, Pallas kernels, local(): pl.pallas_call(kernel, out_shape=jax.ShapeDtypeStruct((T, D), BF), in_spe...  139 us

profile of v7, /device:TPU:0, one launch (start us, length us, event | category | flops | bytes accessed | tf_op | source)
XLA Modules:
  0.0 141.3 jit_solution(688541763551015331)
XLA Ops:
  0.0 139.0 %shard_map.64 = bf16[256,2048]{1,0:T(8,128)(2,1)} custom-call(bf16[256,2048]{1,0:T(8,128)(2,1)} %x_hbm.1, bf16[2048,128]{1,0:T(8,128)(2,1)} %wr_hbm.1, s32[8,256]{1,0:T(8,128)} %bitcast.1, bf16[16,2048,768]{2,1,0:T(8,128)(2,1)} %w1_hbm.1, bf16[16,2048,768]{2,1,0:T(8,128)(2,1)} %w3_hbm.1, bf16[16,768,2048]{2,1,0:T(8,128)(2,1)} %w2_hbm.1), custom_call_target="tpu_custom_call" | custom-call | tf_op jit(solution)/shard_map/pallas_call | solution.py:441
  139.0 2.3 %copy.8 = bf16[256,2048]{1,0:T(8,128)(2,1)} copy(bf16[256,2048]{1,0:T(8,128)(2,1)} %shard_map.64) | data formatting | bytes 2097152

commit v8 on v7

--- a/solution.py
+++ b/solution.py
@@ -222,26 +222,27 @@
     own(2)
     own(3)
     pl.loop(4, 8)(weigh)
-    diag(0)
-    diag(1)
-    arrived(0)
-    arrived(1)
-
-    def gather(q):
+
+    def gather(u, s):
         for r in range(8):
-            for s in range(2):
-                v = _dot(HT[r], X[(2 * q + s) * 8 + r])
-                XIN[:, r * C:(r + 1) * C, s * U:(s + 1) * U] = v.astype(BF).reshape(EL, C, U)
+            v = _dot(HT[r], X[u * 8 + r])
+            XIN[:, r * C:(r + 1) * C, s * U:(s + 1) * U] = v.astype(BF).reshape(EL, C, U)
 
     def tiles(n):
         for i in range(UE):
             for m in range(2):
                 wtload(n + i, m).wait()
 
+    diag(0)
+    arrived(0)
+    diag(1)
+    gather(0, 0)
+    arrived(1)
+
     @pl.loop(0, NQ - 1)
     def _(q):
         u = 2 * q + 2
-        gather(q)
+        gather(u - 1, 1)
         fwd(u)
 
         @pl.when(u + 2 < NU)
@@ -273,17 +274,13 @@
                     wtload(n + NWT + i, m).start()
 
         diag(u + 1)
+        sent(u - 2)
+        sent(u - 1)
         arrived(u)
+        gather(u, 0)
         arrived(u + 1)
 
-    gather(NQ - 1)
-
-    @pl.loop(0, NU)
-    def _(u):
-        sent(u)
-
-    for r in range(1, 8):
-        ecopy(r).wait_send()
+    gather(NU - 1, 1)
 
     @pl.loop(0, EL // UE)
     def _(g):
@@ -386,6 +383,13 @@
             total(0, ())
             for i in range(4):
                 d2d(b, i).wait_send()
+
+            @pl.when(b == 0)
+            def _():
+                sent(NU - 2)
+                sent(NU - 1)
+                for r in range(1, 8):
+                    ecopy(r).wait_send()
 
             @pl.when(b + 2 < NB)
             def _():

time: 141 us -> 140 us (level)
  no operation moved by 1% of the time
where the time goes in v8:
time: 140 us
  Pallas kernels  138 us (99%)
  local copies, waits for them, and re-layouts  2.3 us (2%)
    pallas_call x1, Pallas kernels, local(): pl.pallas_call(kernel, out_shape=jax.ShapeDtypeStruct((T, D), BF), in_spe...  138 us

profile of v8, /device:TPU:0, one launch (start us, length us, event | category | flops | bytes accessed | tf_op | source)
XLA Modules:
  0.0 140.0 jit_solution(7403263251875943238)
XLA Ops:
  0.0 137.7 %shard_map.64 = bf16[256,2048]{1,0:T(8,128)(2,1)} custom-call(bf16[256,2048]{1,0:T(8,128)(2,1)} %x_hbm.1, bf16[2048,128]{1,0:T(8,128)(2,1)} %wr_hbm.1, s32[8,256]{1,0:T(8,128)} %bitcast.1, bf16[16,2048,768]{2,1,0:T(8,128)(2,1)} %w1_hbm.1, bf16[16,2048,768]{2,1,0:T(8,128)(2,1)} %w3_hbm.1, bf16[16,768,2048]{2,1,0:T(8,128)(2,1)} %w2_hbm.1), custom_call_target="tpu_custom_call" | custom-call | tf_op jit(solution)/shard_map/pallas_call | solution.py:445
  137.7 2.3 %copy.8 = bf16[256,2048]{1,0:T(8,128)(2,1)} copy(bf16[256,2048]{1,0:T(8,128)(2,1)} %shard_map.64) | data formatting | bytes 2097152

commit v9 on v8

--- a/solution.py
+++ b/solution.py
@@ -250,8 +250,7 @@
             own(u + 2)
 
 
-        @pl.loop(0, EL // UE)
-        def _(g):
+        for g in range(EL // UE):
             n = q * EL + g * UE
             tiles(n)
             for i in range(UE):
@@ -260,8 +259,7 @@
                 for m in range(2):
                     for f in range(NF):
                         ACC[(e * 2 + m) * NF + f] += _dot(xe, WT[s, m, :, f * U:(f + 1) * U])
-            @pl.when(g == 1)
-            def _():
+            if g == 1:
                 diag(u)
                 fwd(u + 1)
 
@@ -282,8 +280,7 @@
 
     gather(NU - 1, 1)
 
-    @pl.loop(0, EL // UE)
-    def _(g):
+    for g in range(EL // UE):
         n = (NQ - 1) * EL + g * UE
         tiles(n)
         for i in range(UE):
@@ -293,15 +290,11 @@
                 a = ACC[e * 2 * NF + f] + _dot(xe, WT[s, 0, :, f * U:(f + 1) * U])
                 b = ACC[(e * 2 + 1) * NF + f] + _dot(xe, WT[s, 1, :, f * U:(f + 1) * U])
                 X[e * NF + f] = (jax.nn.silu(a) * b).astype(BF)
-
-        @pl.when(n + NWT < NQ * EL)
-        def _():
+        if n + NWT < NQ * EL:
             for i in range(UE):
                 for m in range(2):
                     wtload(n + NWT + i, m).start()
-
-        @pl.when((g == 1) | (g == 2))
-        def _():
+        elif g == 1 or g == 2:
             for i in range(2 * UE):
                 w2start(0, (g - 1) * 2 * UE + i)
                 w2start(1, (g - 1) * 2 * UE + i)

time: 140 us -> 140 us (level)
  no operation moved by 1% of the time
where the time goes in v9:
time: 140 us
  Pallas kernels  137 us (98%)
  local copies, waits for them, and re-layouts  2.3 us (2%)
    pallas_call x1, Pallas kernels, local(): pl.pallas_call(kernel, out_shape=jax.ShapeDtypeStruct((T, D), BF), in_spe...  137 us

profile of v9, /device:TPU:0, one launch (start us, length us, event | category | flops | bytes accessed | tf_op | source)
XLA Modules:
  0.0 139.6 jit_solution(2853036247514542909)
XLA Ops:
  0.0 137.3 %shard_map.64 = bf16[256,2048]{1,0:T(8,128)(2,1)} custom-call(bf16[256,2048]{1,0:T(8,128)(2,1)} %x_hbm.1, bf16[2048,128]{1,0:T(8,128)(2,1)} %wr_hbm.1, s32[8,256]{1,0:T(8,128)} %bitcast.1, bf16[16,2048,768]{2,1,0:T(8,128)(2,1)} %w1_hbm.1, bf16[16,2048,768]{2,1,0:T(8,128)(2,1)} %w3_hbm.1, bf16[16,768,2048]{2,1,0:T(8,128)(2,1)} %w2_hbm.1), custom_call_target="tpu_custom_call" | custom-call | tf_op jit(solution)/shard_map/pallas_call | solution.py:438
  137.3 2.3 %copy.8 = bf16[256,2048]{1,0:T(8,128)(2,1)} copy(bf16[256,2048]{1,0:T(8,128)(2,1)} %shard_map.64) | data formatting | bytes 2097152
